TPU v7x, 32 devices: a whole 2x2x4 slice. The times are simulated.
32 devices in a mesh: member: 2 (over core), tp: 16 (over z, y, x).
Axes of the slice: x: 2, y: 2, z: 4, core: 2. Of those that a mesh axis runs over, the one named last changes fastest.
Arguments:
- stream_in: bfloat16 [512, 4096], P(('member', 'tp')), may hold values from -6 to 6
- kv_cache: bfloat16 [512, 512, 2048], P(('member', 'tp')), may hold values from -400 to 400
- lengths: int32 [128], replicated, may hold values from 1 to 512
- targets: int32 [128], replicated, may hold values from 0 to 65535
- norm_gains: float32 [3, 4096], replicated, may hold values from 0.1 to 1.9
- w_qkv: bfloat16 [4096, 6144], P(None, 'tp'), may hold values from -0.09375 to 0.09375
- w_out: bfloat16 [4096, 4096], P('tp'), may hold values from -0.09375 to 0.09375
- w_gate_up: bfloat16 [2, 4096, 14336], P(None, None, 'tp'), may hold values from -0.09375 to 0.09375
- w_down: bfloat16 [14336, 4096], P('tp'), may hold values from -0.046875 to 0.046875
- lm_head: bfloat16 [4096, 65536], P(None, 'tp'), may hold values from -300 to 300
- fast_in: float32 [4, 2, 4096], P('member'), may hold values from 0.1 to 1.9
- fast_hidden: float32 [4, 3, 14336], P('member', None, 'tp'), may hold values from 0.1 to 1.9
- fast_out: float32 [4, 4096], P('member'), may hold values from 0.1 to 1.9
Outputs:
- mean_logits: bfloat16 [128, 65536], P(None, 'tp')
- token_logprob: float32 [128], replicated
Inputs may be any that keep to these rules, and one draw needn't show every extreme that they name: lengths is the same for all members.
All inputs are finite; a program needn't handle non-finite values.
Results may differ from a plain program's by a relative error of at most 0.02.
Values may be sent and summed in bfloat16 or wider, within the bound.
A program may use at most 192 MiB of HBM per device.

v0:
```python
import jax
import jax.numpy as jnp
from jax import lax
from jax.sharding import PartitionSpec as P

HEADS = 32
KV = 8
HD = 128
CACHE = 512


ROPE_BASE = 500000.0


def rms_norm(values_in, gain):
    return (
        values_in
        * lax.rsqrt(jnp.mean(values_in * values_in, axis=-1, keepdims=True) + 1e-05)
        * gain
    )


def rotate(values_in, positions):
    half_dim = values_in.shape[-1] // 2
    frequency = ROPE_BASE ** (-jnp.arange(half_dim, dtype=jnp.float32) * 2.0 / values_in.shape[-1])
    angles = positions.astype(jnp.float32)[:, None, None] * frequency[None, None, :]
    lower_half = values_in[..., :half_dim]
    upper_half = values_in[..., half_dim:]
    return jnp.concatenate(
        [
            lower_half * jnp.cos(angles) - upper_half * jnp.sin(angles),
            upper_half * jnp.cos(angles) + lower_half * jnp.sin(angles),
        ],
        axis=-1,
    )


def attend(projected, cache_rows, positions):
    row_count = projected.shape[0]
    head_cols = HEADS * HD
    kv_cols = KV * HD
    queries = rotate(
        projected[:, :head_cols].astype(jnp.float32).reshape(row_count, HEADS, HD), positions
    ).astype(jnp.bfloat16)
    new_key = rotate(
        projected[:, head_cols : head_cols + kv_cols]
        .astype(jnp.float32)
        .reshape(row_count, KV, HD),
        positions,
    ).astype(jnp.bfloat16)
    new_value = projected[:, head_cols + kv_cols :].reshape(row_count, KV, HD)
    cache_keys = cache_rows[:, :, :kv_cols].reshape(row_count, CACHE, KV, HD)
    cache_values = cache_rows[:, :, kv_cols:].reshape(row_count, CACHE, KV, HD)
    grouped = queries.reshape(row_count, KV, HEADS // KV, HD)
    inv_root = HD ** (-0.5)
    cached = (
        jnp.einsum("rkgd,rckd->rkgc", grouped, cache_keys, preferred_element_type=jnp.float32)
        * inv_root
    )
    fresh = (
        jnp.einsum("rkgd,rkd->rkg", grouped, new_key, preferred_element_type=jnp.float32) * inv_root
    )
    in_cache = jnp.arange(CACHE)[None, :] < positions[:, None]
    cached = jnp.where(in_cache[:, None, None, :], cached, -1e30)
    peak = jnp.maximum(jnp.max(cached, axis=-1), fresh)
    weights = jnp.exp(cached - peak[..., None])
    fresh_w = jnp.exp(fresh - peak)
    total_sum = jnp.sum(weights, axis=-1) + fresh_w
    probs = (weights / total_sum[..., None]).astype(jnp.bfloat16)
    fresh_p = (fresh_w / total_sum).astype(jnp.bfloat16)
    result = jnp.einsum("rkgc,rckd->rkgd", probs, cache_values, preferred_element_type=jnp.float32)
    result = (
        result
        + fresh_p.astype(jnp.float32)[..., None] * new_value.astype(jnp.float32)[:, :, None, :]
    )
    return result.reshape(row_count, HEADS * HD).astype(jnp.bfloat16)


def body(
    stream_in,
    kv_cache,
    lengths,
    targets,
    norm_gains,
    w_qkv,
    w_out,
    w_gate_up,
    w_down,
    lm_head,
    fast_in,
    fast_hidden,
    fast_out,
):
    tp_count = lax.axis_size("tp")
    tp_rank = lax.axis_index("tp")
    mem_dev = fast_in.shape[0]
    batch_rows = lengths.shape[0]
    own_rows = stream_in.shape[0]
    all_rows = own_rows * tp_count
    width = stream_in.shape[1]
    first_row = tp_rank * own_rows
    positions = lax.dynamic_slice_in_dim(lengths, first_row % batch_rows, own_rows, 0)
    own_member = first_row // batch_rows
    own_scale = lax.dynamic_index_in_dim(fast_out, own_member, 0, keepdims=True)
    own_normed = rms_norm(stream_in.astype(jnp.float32), norm_gains[0]).astype(jnp.bfloat16)
    attn_in = lax.all_gather(own_normed, "tp", axis=0, tiled=True)
    projected = jnp.dot(attn_in, w_qkv, preferred_element_type=jnp.float32).astype(jnp.bfloat16)
    row_major = lax.all_to_all(projected, "tp", split_axis=0, concat_axis=1, tiled=True)
    attended = attend(row_major, kv_cache, positions)
    head_major = lax.all_to_all(attended, "tp", split_axis=1, concat_axis=0, tiled=True)
    picked = head_major
    attn_sum = lax.psum_scatter(
        jnp.dot(picked, w_out, preferred_element_type=jnp.float32),
        "tp",
        scatter_dimension=0,
        tiled=True,
    )
    middle = (stream_in.astype(jnp.float32) + attn_sum).astype(jnp.bfloat16)
    own_ffn = rms_norm(middle.astype(jnp.float32), norm_gains[1]).astype(jnp.bfloat16)
    ffn_in = lax.all_gather(own_ffn, "tp", axis=0, tiled=True)
    grouped = ffn_in.astype(jnp.float32).reshape(mem_dev, batch_rows, width)
    gate_in = (grouped * fast_in[:, 0][:, None, :]).astype(jnp.bfloat16).reshape(all_rows, width)
    up_in = (grouped * fast_in[:, 1][:, None, :]).astype(jnp.bfloat16).reshape(all_rows, width)
    hidden_cols = w_gate_up.shape[2]
    gate_act = (
        jnp.dot(gate_in, w_gate_up[0], preferred_element_type=jnp.float32).reshape(
            mem_dev, batch_rows, hidden_cols
        )
        * fast_hidden[:, 0][:, None, :]
    )
    up_act = (
        jnp.dot(up_in, w_gate_up[1], preferred_element_type=jnp.float32).reshape(
            mem_dev, batch_rows, hidden_cols
        )
        * fast_hidden[:, 1][:, None, :]
    )
    hidden = (
        (jax.nn.silu(gate_act) * up_act * fast_hidden[:, 2][:, None, :])
        .astype(jnp.bfloat16)
        .reshape(all_rows, hidden_cols)
    )
    picked = hidden
    down_sum = lax.psum_scatter(
        jnp.dot(picked, w_down, preferred_element_type=jnp.float32),
        "tp",
        scatter_dimension=0,
        tiled=True,
    )
    layer_out = (middle.astype(jnp.float32) + down_sum * own_scale).astype(jnp.bfloat16)
    own_final = rms_norm(layer_out.astype(jnp.float32), norm_gains[2]).astype(jnp.bfloat16)
    final_in = lax.all_gather(own_final, "tp", axis=0, tiled=True)
    logits = jnp.dot(final_in, lm_head, preferred_element_type=jnp.float32)
    vocab_cols = lm_head.shape[1]
    member_total = jnp.sum(logits.reshape(mem_dev, batch_rows, vocab_cols), axis=0)
    member_count = mem_dev * lax.axis_size("member")
    mean_logit = (
        lax.psum(member_total.astype(jnp.bfloat16), "member").astype(jnp.float32) / member_count
    )
    column_ids = tp_rank * vocab_cols + jnp.arange(vocab_cols)
    target_part = jnp.sum(
        jnp.where(column_ids[None, :] == targets[:, None], mean_logit, 0.0), axis=-1
    )
    local_peak = jnp.max(mean_logit, axis=-1)
    peak = lax.pmax(local_peak, "tp")
    exp_total, target_logit = lax.psum(
        (jnp.sum(jnp.exp(mean_logit - peak[:, None]), axis=-1), target_part), "tp"
    )
    token_logprob = target_logit - (peak + jnp.log(exp_total))
    return (mean_logit.astype(jnp.bfloat16), token_logprob)


def solution(mesh):
    in_specs = (
        P(("member", "tp"), None),
        P(("member", "tp"), None, None),
        P(),
        P(),
        P(),
        P(None, "tp"),
        P("tp", None),
        P(None, None, "tp"),
        P("tp", None),
        P(None, "tp"),
        P("member", None, None),
        P("member", None, "tp"),
        P("member", None),
    )
    out_specs = (P(None, "tp"), P())
    return jax.shard_map(body, mesh=mesh, in_specs=in_specs, out_specs=out_specs, check_vma=False)
```

profile of v0, /device:TPU:0, one launch (start us, length us, event | category | flops | bytes accessed | tf_op | source)
XLA Modules:
  0.0 622.7 jit_solution(10672102106241271460)
XLA Ops:
  7.2 0.0 copy-start
  7.2 0.0 all-gather.4.cloned.1.call-start
  7.2 1.7 fusion.49
  8.9 1.0 fusion.33
  10.0 1.7 fusion.35
  11.6 0.0 all-gather.4.cloned.1.call-update
  11.7 0.7 fusion.47
  12.4 23.1 %fusion.48 = (bf16[16,512,1024]{2,1,0:T(8,128)(2,1)}, bf16[16,512,1024]{2,1,0:T(8,128)(2,1)}) fusion(bf16[16,512,2048]{2,1,0:T(8,128)(2,1)} %param.14), kind=kLoop, calls=%fused_computation.81 | loop fusion | bytes 67108864 | tf_op jit(solution)/shard_map/slice | solution.py:52
  35.5 39.4 %all-gather.4.cloned.1.call-done = bf16[256,4096]{1,0:T(8,128)(2,1)} async-done(((bf16[16,4096]{1,0:T(8,128)(2,1)}), bf16[256,4096]{1,0:T(8,128)(2,1)}) %all-gather.4.cloned.1.call-update) | async-done | bytes 2097168 | tf_op jit(solution)/shard_map/all_gather | solution.py:106
  74.9 3.5 convolution_convert_fusion
  78.5 4.4 all-to-all-start
  82.9 0.0 reduce-scatter.3.cloned.1.call-start
  82.9 0.1 iota_compare_fusion
  83.0 21.6 %copy.34 = bf16[16,512,1024]{1,2,0:T(8,128)(2,1)} copy(bf16[16,512,1024]{2,1,0:T(8,128)(2,1)} %get-tuple-element.13) | data formatting | bytes 33554432
  104.6 21.6 %copy.33 = bf16[16,512,1024]{1,2,0:T(8,128)(2,1)} copy(bf16[16,512,1024]{2,1,0:T(8,128)(2,1)} %get-tuple-element.12) | data formatting | bytes 33554432
  126.3 0.1 multiply_cosine_fusion
  126.4 0.0 all-to-all-done
  126.5 0.1 copy.36
  126.6 0.1 subtract_convert_fusion
  126.7 0.1 subtract_convert_fusion.1
  126.8 0.1 maximum_bitcast_fusion
  126.9 0.3 fusion.41
  127.3 8.2 %fusion.51 = (f32[16,8,4]{2,1,0:T(8,128)S(1)}, f32[16,8,4,512]{3,2,1,0:T(4,128)S(1)}) fusion(bf16[16,512,8,128]{1,3,2,0:T(8,128)(2,1)} %bitcast.76, bf16[16,8,4,64]{3,2,1,0:T(4,128)(2,1)S(1)} %bitcast.92, bf16[16,8,4,64]{3,2,1,0:T(4,128)(2,1)S(1)} %bitcast.90, pred[16,512]{1,0:T(8,128)(4,1)S(1)} %iota_compare_fusion), kind=kOutput, calls=%fused_computation.84 | convolution fusion | flops 68156928 | bytes 17967104 | tf_op jit(solution)/shard_map/rkgd,rckd->rkgc/dot_general | solution.py:57
  135.5 0.7 fusion.27
  136.2 0.0 copy-start.2
  136.3 8.4 %fusion.26 = bf16[16,8,4,128]{3,2,1,0:T(4,128)(2,1)S(1)} fusion(bf16[16,512,8,128]{1,3,2,0:T(8,128)(2,1)} %bitcast.77, f32[16,8,4,512]{3,2,1,0:T(4,128)S(1)} %get-tuple-element.36, f32[16,8,4]{2,1,0:T(8,128)S(1)} %get-tuple-element.20, f32[16,8,4]{2,1,0:T(8,128)S(1)} %multiply_maximum_fusion, f32[16,8,128]{2,1,0:T(8,128)S(1)} %bitcast.97, ...), kind=kOutput, calls=%fused_computation.24 | convolution fusion | flops 68091904 | bytes 18028544 | tf_op jit(solution)/shard_map/rkgc,rckd->rkgd/dot_general | solution.py:71
  144.7 0.1 convert_element_type.97
  144.8 14.5 %all_to_all.35 = bf16[16,16,256]{2,0,1:T(8,128)(2,1)S(1)} all-to-all(bf16[16,16,256]{2,0,1:T(8,128)(2,1)S(1)} %copy.26), channel_id=1, replica_groups=mesh['member'=2,'tp'=16] {'tp'}, dimensions={1} | all-to-all | bytes 262144 | tf_op jit(solution)/shard_map/all_to_all | solution.py:110
  159.3 2.7 fusion.52
  162.0 0.0 reduce-scatter.3.cloned.1.call-update
  162.0 0.0 all-gather.6.cloned.1.call-start
  162.1 92.5 %reduce-scatter.3.cloned.1.call-done = f32[16,4096]{1,0:T(8,128)} async-done(((f32[256,4096]{1,0:T(8,128)}), f32[16,4096]{1,0:T(8,128)}) %reduce-scatter.3.cloned.1.call-update) | async-done | bytes 262160 | tf_op jit(solution)/shard_map/reduce_scatter | solution.py:112
  254.6 1.1 fusion.37
  255.7 0.8 fusion.39
  256.5 0.0 all-gather.6.cloned.1.call-update
  256.5 0.2 reduce-scatter.5.cloned.1.call-start
  256.8 0.1 fusion.50
  256.8 0.1 copy_bitcast_fusion
  256.9 61.0 %all-gather.6.cloned.1.call-done = bf16[256,4096]{1,0:T(8,128)(2,1)} async-done(((bf16[16,4096]{1,0:T(8,128)(2,1)}), bf16[256,4096]{1,0:T(8,128)(2,1)}) %all-gather.6.cloned.1.call-update) | async-done | bytes 2097168 | tf_op jit(solution)/shard_map/all_gather | solution.py:120
  317.9 2.3 fusion.6
  320.1 0.0 slice-start
  320.2 5.6 fusion.11
  325.8 0.0 slice-start.1
  325.8 5.6 fusion.23
  331.5 4.4 fusion.53
  335.8 0.0 reduce-scatter.5.cloned.1.call-update
  335.9 0.0 all-gather.8.cloned.1.call-start
  335.9 0.7 copy-done.7
  336.6 93.5 %reduce-scatter.5.cloned.1.call-done = f32[16,4096]{1,0:T(8,128)} async-done(((f32[256,4096]{1,0:T(8,128)}), f32[16,4096]{1,0:T(8,128)}) %reduce-scatter.5.cloned.1.call-update) | async-done | bytes 262160 | tf_op jit(solution)/shard_map/reduce_scatter | solution.py:143
  430.1 1.1 fusion.30
  431.2 0.8 fusion.32
  432.0 0.0 all-gather.8.cloned.1.call-update
  432.0 0.0 all-reduce.3.cloned.1.call-start
  432.0 61.2 %all-gather.8.cloned.1.call-done = bf16[256,4096]{1,0:T(8,128)(2,1)} async-done(((bf16[16,4096]{1,0:T(8,128)(2,1)}), bf16[256,4096]{1,0:T(8,128)(2,1)}) %all-gather.8.cloned.1.call-update) | async-done | bytes 2097168 | tf_op jit(solution)/shard_map/all_gather | solution.py:151
  493.2 16.9 %fusion.54 = f32[256,4096]{1,0:T(8,128)} fusion(bf16[256,4096]{1,0:T(8,128)(2,1)} %all-gather.8.cloned.1.call-done, bf16[4096,4096]{1,0:T(8,128)(2,1)} %param.22), kind=kOutput, calls=%fused_computation.87 | convolution fusion | flops 8589934592 | bytes 39845888 | tf_op jit(solution)/shard_map/dot_general | solution.py:152
  510.1 3.9 reduce_sum.67
  514.0 0.0 all-reduce.3.cloned.1.call-update
  514.1 18.4 %all-reduce.3.cloned.1.call-done = bf16[128,4096]{1,0:T(8,128)(2,1)} async-done(((bf16[128,4096]{1,0:T(8,128)(2,1)}), bf16[128,4096]{1,0:T(8,128)(2,1)}) %all-reduce.3.cloned.1.call-update) | async-done | bytes 1048592 | tf_op jit(solution)/shard_map/psum | solution.py:157
  532.5 1.5 fusion.8
  534.0 42.0 %pmax.7 = f32[128]{0:T(128)S(1)} all-reduce(f32[128]{0:T(128)S(1)} %fusion.8), channel_id=1, replica_groups=mesh['member'=2,'tp'=16] {'tp'}, use_global_device_ids=true, to_apply=%region_12.13 | all-reduce | flops 128 | bytes 1024 | tf_op jit(solution)/shard_map/pmax | solution.py:164
  576.0 2.9 exponential_reduce_fusion
  578.8 36.5 %all-reduce = (f32[128]{0:T(128)S(1)}, f32[128]{0:T(128)S(1)}) all-reduce(f32[128]{0:T(128)S(1)} %get-tuple-element.3, f32[128]{0:T(128)S(1)} %get-tuple-element.2), channel_id=1, replica_groups=mesh['member'=2,'tp'=16] {'tp'}, use_global_device_ids=true, to_apply=%region_10.11 | all-reduce | flops 256 | bytes 2048 | tf_op jit(solution)/shard_map/psum | solution.py:165
  615.4 0.5 add_subtract_fusion
  615.9 0.0 copy-done.1
  (32 shorter events, 0.3 us)
Async XLA Ops:
  7.2 67.8 %copy-start = (bf16[4096,384]{1,0:T(8,128)(2,1)S(1)}, bf16[4096,384]{1,0:T(8,128)(2,1)}, u32[]{:S(2)}) copy-start(bf16[4096,384]{1,0:T(8,128)(2,1)} %param.18) | copy-start | bytes 9437188
  7.2 67.7 %all-gather.4.cloned.1.call-start = ((), (), s32[]{:S(2)}) async-start(), calls=%async_computation.4 | async-start | bytes 2228224 | tf_op jit(solution)/shard_map/all_gather | solution.py:106
  78.5 47.9 %all-to-all-start = ((bf16[16,16,384]{2,1,0:T(8,128)(2,1)}), bf16[16,16,384]{2,1,0:T(8,128)(2,1)S(1)}, u32[]{:S(2)}, u32[]{:S(2)}) async-start(bf16[16,16,384]{2,1,0:T(8,128)(2,1)} %bitcast.1), calls=%async_computation | async-start | bytes 393216 | tf_op jit(solution)/shard_map/all_to_all | solution.py:108
  82.9 171.7 %reduce-scatter.3.cloned.1.call-start = ((), (), s32[]{:S(2)}) async-start(), calls=%async_computation.5 | async-start | bytes 4456448 | tf_op jit(solution)/shard_map/reduce_scatter | solution.py:112
  136.2 23.1 %copy-start.2 = (bf16[256,4096]{1,0:T(8,128)(2,1)S(1)}, bf16[256,4096]{1,0:T(8,128)(2,1)}, u32[]{:S(2)}) copy-start(bf16[256,4096]{1,0:T(8,128)(2,1)} %param.19) | copy-start | bytes 6291460
  159.3 95.3 %copy-start.3 = (bf16[16,4096]{1,0:T(8,128)(2,1)S(1)}, bf16[16,4096]{1,0:T(8,128)(2,1)}, u32[]{:S(2)}) copy-start(bf16[16,4096]{1,0:T(8,128)(2,1)} %param.13) | copy-start | bytes 393220
  159.3 96.4 %copy-start.5 = (f32[1,4096]{1,0:T(1,128)S(1)}, f32[1,4096]{1,0:T(1,128)}, u32[]{:S(2)}) copy-start(f32[1,4096]{1,0:T(1,128)} %get-tuple-element.27) | copy-start | bytes 49156
  159.3 97.4 %copy-start.6 = (f32[2,3,896]{2,0,1:T(2,128)S(1)}, f32[2,3,896]{2,0,1:T(2,128)}, u32[]{:S(2)}) copy-start(f32[2,3,896]{2,0,1:T(2,128)} %param.24) | copy-start | bytes 64516
  162.0 94.8 %copy-start.4 = (f32[2,2,4096]{2,1,0:T(2,128)S(1)}, f32[2,2,4096]{2,1,0:T(2,128)}, u32[]{:S(2)}) copy-start(f32[2,2,4096]{2,1,0:T(2,128)} %param.23) | copy-start | bytes 196612
  162.0 155.9 %all-gather.6.cloned.1.call-start = ((), (), s32[]{:S(2)}) async-start(), calls=%async_computation.6 | async-start | bytes 2228224 | tf_op jit(solution)/shard_map/all_gather | solution.py:120
  256.5 173.6 %reduce-scatter.5.cloned.1.call-start = ((), (), s32[]{:S(2)}) async-start(), calls=%async_computation.7 | async-start | bytes 4456448 | tf_op jit(solution)/shard_map/reduce_scatter | solution.py:143
  320.1 11.3 %slice-start = ((s8[7340032]{0:T(1024)(128)(4,1)}), s8[4194304]{0:T(1024)(128)(4,1)S(1)}, s32[]{:S(2)}) async-start(s8[7340032]{0:T(1024)(128)(4,1)} %bitcast.78), calls=%async_computation.10 | async-start | bytes 8388608
  325.8 5.7 slice-start.1
  335.8 0.8 copy-start.7
  335.9 157.3 %all-gather.8.cloned.1.call-start = ((), (), s32[]{:S(2)}) async-start(), calls=%async_computation.8 | async-start | bytes 2228224 | tf_op jit(solution)/shard_map/all_gather | solution.py:151
  432.0 100.5 %all-reduce.3.cloned.1.call-start = ((), (), s32[]{:S(2)}) async-start(), calls=%async_computation.9 | async-start | bytes 2097152 | tf_op jit(solution)/shard_map/psum | solution.py:157
  510.1 65.8 %copy-start.8 = (s32[128]{0:T(128)S(1)}, s32[128]{0:T(128)}, u32[]{:S(2)}) copy-start(s32[128]{0:T(128)} %param.16) | copy-start | bytes 1540
  510.1 105.8 %copy-start.1 = (bf16[4096,384]{1,0:T(8,128)(2,1)S(1)}, bf16[4096,384]{1,0:T(8,128)(2,1)}, u32[]{:S(2)}) copy-start(bf16[4096,384]{1,0:T(8,128)(2,1)} %param.18) | copy-start | bytes 9437188
Sparse Core Ops, SparseCore 0:
  11.8 63.0 all-gather.3
  162.1 92.4 reduce-scatter.2
  257.9 59.8 all-gather.5
  336.0 94.0 reduce-scatter.4
  433.3 59.8 all-gather.7
  514.2 18.2 all-reduce.2
where the time goes:
time: 624 us; the launch traced here: 623 us
  waiting for transfers between devices  366 us (59%)
  blocking collectives  93 us (15%)
  local copies, waits for them, and re-layouts  69.1 us (11%)
  matrix products  55.7 us (9%)
  other arithmetic  19.6 us (3%)
  between operations  14.4 us (2%)
    reduce_scatter x1, waiting for transfers between devices, body(): lax.psum_scatter(jnp.dot(picked, w_down, preferred_element_type=jnp.float...  93.5 us
    reduce_scatter x1, waiting for transfers between devices, body(): lax.psum_scatter(jnp.dot(picked, w_out, preferred_element_type=jnp.float3...  92.5 us
    all_gather x1, waiting for transfers between devices, body(): final_in = lax.all_gather(own_final, 'tp', axis=0, tiled=True)  61.2 us
    all_gather x1, waiting for transfers between devices, body(): ffn_in = lax.all_gather(own_ffn, 'tp', axis=0, tiled=True)  61 us
    unnamed x28, local copies, waits for them, and re-layouts  44.1 us
    pmax x1, blocking collectives, body(): peak = lax.pmax(local_peak, 'tp')  42 us
    all_gather x1, waiting for transfers between devices, body(): attn_in = lax.all_gather(own_normed, 'tp', axis=0, tiled=True)  39.4 us
    psum x1, blocking collectives, body(): lax.psum((jnp.sum(jnp.exp(mean_logit - peak[:, None]), axis=-1), target_p...  36.5 us
  transfers between devices with their start and end apart: 7, of which 6 were waited for; matrix products, arithmetic and copies ran while one was open for 11% of the time, Pallas kernels for 0%

commit v1 on v0

--- a/solution.py
+++ b/solution.py
@@ -1,6 +1,10 @@
+import functools
+
 import jax
 import jax.numpy as jnp
 from jax import lax
+from jax.experimental import pallas as pl
+from jax.experimental.pallas import tpu as pltpu
 from jax.sharding import PartitionSpec as P
 
 HEADS = 32
@@ -76,7 +80,7 @@
     return result.reshape(row_count, HEADS * HD).astype(jnp.bfloat16)
 
 
-def body(
+def plain_body(
     stream_in,
     kv_cache,
     lengths,
@@ -169,6 +173,555 @@
     return (mean_logit.astype(jnp.bfloat16), token_logprob)
 
 
+BF16 = jnp.bfloat16
+F32 = jnp.float32
+DMA = pltpu.SemaphoreType.DMA
+QUAD = 4
+
+
+def norm_rows(values_in, gain):
+    return (
+        values_in
+        * lax.rsqrt(jnp.mean(values_in * values_in, axis=-1, keepdims=True) + 1e-05)
+        * gain
+    )
+
+
+class Place:
+    def __init__(self, lines):
+        self.tp = lax.axis_index("tp")
+        self.member = lax.axis_index("member")
+        self.lines = lines
+        self.quad = lax.rem(self.tp, QUAD)
+        self.line = self.tp // QUAD
+        self.quad_x = self.quad + 1 - 2 * lax.rem(self.quad, 2)
+        self.quad_y = lax.rem(self.quad + 2, QUAD)
+        self.quad_d = self.quad_x + self.quad_y - self.quad
+        self.to_x = {"tp": self.line * QUAD + self.quad_x}
+        self.to_y = {"tp": self.line * QUAD + self.quad_y}
+
+    def line_at(self, step):
+        return lax.rem(self.line + step + self.lines, self.lines)
+
+    def to_line(self, step):
+        return {"tp": self.line_at(step) * QUAD + self.quad}
+
+
+def remote(src, dst, send_sem, recv_sem, device):
+    copy = pltpu.make_async_remote_copy(
+        src_ref=src,
+        dst_ref=dst,
+        send_sem=send_sem,
+        recv_sem=recv_sem,
+        device_id=device,
+        device_id_type=pl.DeviceIdType.MESH,
+    )
+    copy.start()
+    return copy
+
+
+def greet(devices):
+    barrier = pltpu.get_barrier_semaphore()
+    for device in devices:
+        pl.semaphore_signal(
+            barrier, inc=1, device_id=device, device_id_type=pl.DeviceIdType.MESH
+        )
+    pl.semaphore_wait(barrier, len(devices))
+
+
+def gather_rows(place, own, out, sems, line_steps, block_of):
+    local_sem, sends, recvs = sems
+    rows, cols = own.shape
+    half = cols // 2
+
+    def rows_of(step, quad):
+        return pl.ds(pl.multiple_of(block_of(step, quad) * rows, rows), rows)
+
+    mine = out.at[rows_of(0, place.quad)]
+    local = pltpu.make_async_copy(own, mine, local_sem)
+    local.start()
+    line_copies = []
+    for k, step in enumerate(line_steps):
+        if k:
+            line_copies.append(
+                remote(own, mine, sends.at[0, k], recvs.at[0, k], place.to_line(step))
+            )
+        else:
+            line_copies.append(None)
+    by_x, by_y, over_x, over_y = [], [], [], []
+
+    def spread(k):
+        block = own if k == 0 else out.at[rows_of(-line_steps[k], place.quad)]
+        into = out.at[rows_of(-line_steps[k], place.quad)]
+        by_x.append(remote(block, into, sends.at[1, k], recvs.at[1, k], place.to_x))
+        by_y.append(remote(block, into, sends.at[2, k], recvs.at[2, k], place.to_y))
+
+    def relay(k):
+        by_x[k].wait_recv()
+        from_x = out.at[rows_of(-line_steps[k], place.quad_x), pl.ds(0, half)]
+        over_y.append(remote(from_x, from_x, sends.at[3, k], recvs.at[3, k], place.to_y))
+        by_y[k].wait_recv()
+        from_y = out.at[rows_of(-line_steps[k], place.quad_y), pl.ds(half, half)]
+        over_x.append(remote(from_y, from_y, sends.at[4, k], recvs.at[4, k], place.to_x))
+
+    spread(0)
+    for k in range(1, len(line_steps)):
+        line_copies[k].wait_recv()
+        spread(k)
+        relay(k - 1)
+    relay(len(line_steps) - 1)
+    for k in range(len(line_steps)):
+        over_y[k].wait_recv()
+        over_x[k].wait_recv()
+    local.wait()
+    for copies in (line_copies, by_x, by_y, over_x, over_y):
+        for copy in copies:
+            if copy is not None:
+                copy.wait_send()
+
+
+def sum_rows(place, part, sems, bufs):
+    sends, recvs = sems
+    got_dx, got_dy, put_x, put_y, got_x, got_y, put_z, got_z = bufs
+    rows = got_x.shape[1]
+    half = got_dx.shape[2]
+    low, high = pl.ds(0, half), pl.ds(half, half)
+    steps = list(range(1, place.lines)) + [0]
+
+    def rows_of(step, quad):
+        index = place.line_at(step) * QUAD + quad
+        return pl.ds(pl.multiple_of(index * rows, rows), rows)
+
+    d_x, d_y, x_high, y_low, x_low, y_high, z_copies = {}, {}, {}, {}, {}, {}, {}
+    for k in steps:
+        diag = rows_of(k, place.quad_d)
+        d_x[k] = remote(part.at[diag, high], got_dx.at[k], sends.at[0, k], recvs.at[0, k], place.to_x)
+        d_y[k] = remote(part.at[diag, low], got_dy.at[k], sends.at[1, k], recvs.at[1, k], place.to_y)
+    for k in steps:
+        x_high[k] = remote(
+            part.at[rows_of(k, place.quad_x), high], got_x.at[k, :, high],
+            sends.at[2, k], recvs.at[2, k], place.to_x,
+        )
+        y_low[k] = remote(
+            part.at[rows_of(k, place.quad_y), low], got_y.at[k, :, low],
+            sends.at[3, k], recvs.at[3, k], place.to_y,
+        )
+        d_y[k].wait_recv()
+        put_x[k] = (
+            part[rows_of(k, place.quad_x), low].astype(F32) + got_dy[k].astype(F32)
+        ).astype(BF16)
+        x_low[k] = remote(
+            put_x.at[k], got_x.at[k, :, low], sends.at[4, k], recvs.at[4, k], place.to_x
+        )
+        d_x[k].wait_recv()
+        put_y[k] = (
+            part[rows_of(k, place.quad_y), high].astype(F32) + got_dx[k].astype(F32)
+        ).astype(BF16)
+        y_high[k] = remote(
+            put_y.at[k], got_y.at[k, :, high], sends.at[5, k], recvs.at[5, k], place.to_y
+        )
+    total = None
+    for k in steps:
+        for copies in (x_high, y_low, x_low, y_high):
+            copies[k].wait_recv()
+        quad_sum = (
+            part[rows_of(k, place.quad), :].astype(F32)
+            + got_x[k].astype(F32)
+            + got_y[k].astype(F32)
+        )
+        if k:
+            put_z[k] = quad_sum.astype(BF16)
+            z_copies[k] = remote(
+                put_z.at[k], got_z.at[k], sends.at[6, k], recvs.at[6, k], place.to_line(k)
+            )
+        else:
+            total = quad_sum
+    for k in steps[:-1]:
+        z_copies[k].wait_recv()
+        total = total + got_z[k].astype(F32)
+    for copies in (d_x, d_y, x_high, y_low, x_low, y_high, z_copies):
+        for copy in copies.values():
+            copy.wait_send()
+    return total
+
+
+def near(place):
+    return [place.to_x, place.to_y] + [place.to_line(k) for k in range(1, place.lines)]
+
+
+def gather_kernel(lines, stream, gain, out, own, local_sem, sends, recvs):
+    place = Place(lines)
+    own[...] = norm_rows(stream[...].astype(F32), gain[...]).astype(BF16)
+    greet(near(place))
+    gather_rows(
+        place, own, out, (local_sem, sends, recvs), list(range(lines)),
+        lambda step, quad: place.line_at(step) * QUAD + quad,
+    )
+
+
+def middle_kernel(
+    lines, part, stream, gain, middle, out, own, local_sem, sends, recvs, sum_sends, sum_recvs, *bufs
+):
+    place = Place(lines)
+    greet(near(place))
+    total = sum_rows(place, part, (sum_sends, sum_recvs), bufs)
+    middle[...] = (stream[...].astype(F32) + total).astype(BF16)
+    own[...] = norm_rows(middle[...].astype(F32), gain[...]).astype(BF16)
+    gather_rows(
+        place, own, out, (local_sem, sends, recvs), list(range(lines)),
+        lambda step, quad: place.line_at(step) * QUAD + quad,
+    )
+
+
+def final_kernel(
+    lines, part, middle, scale, gain, out,
+    own, away, from_core, pair, from_pair, mean,
+    local_sem, sends, recvs, side_sends, side_recvs, sum_sends, sum_recvs, *bufs
+):
+    place = Place(lines)
+    other = {"member": 1 - place.member}
+    greet(near(place) + [other])
+    total = sum_rows(place, part, (sum_sends, sum_recvs), bufs)
+    layer_out = (middle[...].astype(F32) + total * scale[...]).astype(BF16)
+    normed = norm_rows(layer_out.astype(F32), gain[...]).astype(BF16)
+    half = mean.shape[1]
+    first = place.member == 0
+    low, high = normed[:, :half], normed[:, half:]
+    own[...] = jnp.where(first, low.astype(F32), high.astype(F32))
+    away[...] = jnp.where(first, high.astype(F32), low.astype(F32)).astype(BF16)
+    core = remote(away, from_core, side_sends.at[0], side_recvs.at[0], other)
+    core.wait_recv()
+    own[...] = own[...] + from_core[...].astype(F32)
+    pair[...] = own[...]
+    twin = remote(
+        pair, from_pair, side_sends.at[1], side_recvs.at[1], place.to_line(lines // 2)
+    )
+    twin.wait_recv()
+    mean[...] = ((own[...] + from_pair[...]) * 0.25).astype(BF16)
+    turn = 1 - 2 * lax.rem(place.line, 2)
+
+    class Pairwise:
+        pass
+
+    near_line = Pairwise()
+    near_line.quad, near_line.quad_x, near_line.quad_y = place.quad, place.quad_x, place.quad_y
+    near_line.to_x, near_line.to_y = place.to_x, place.to_y
+    near_line.to_line = lambda step: {"tp": (place.line + turn) * QUAD + place.quad}
+    mine = out.at[place.member]
+    gather_rows(
+        near_line, mean, mine, (local_sem, sends, recvs), [0, 1],
+        lambda step, quad: lax.rem(place.line + abs(step), 2) * QUAD + quad,
+    )
+    share = remote(mine, mine, side_sends.at[2], side_recvs.at[2], other)
+    share.wait_recv()
+    for copy in (core, twin, share):
+        copy.wait_send()
+
+
+VMEM = pl.BlockSpec(memory_space=pltpu.VMEM)
+VMEM_BYTES = 60 * 1024 * 1024
+
+
+def call_linked(kernel, number, out_shape, scratch, args):
+    return pl.pallas_call(
+        kernel,
+        out_shape=out_shape,
+        in_specs=[VMEM] * len(args),
+        out_specs=jax.tree.map(lambda _: VMEM, out_shape),
+        scratch_shapes=scratch,
+        compiler_params=pltpu.CompilerParams(
+            collective_id=number, has_side_effects=True, vmem_limit_bytes=VMEM_BYTES
+        ),
+    )(*args)
+
+
+def gather_scratch(lines):
+    return [DMA, DMA((5, lines)), DMA((5, lines))]
+
+
+def sum_scratch(lines, rows, cols):
+    small = pltpu.VMEM((lines, rows, cols // 2), BF16)
+    large = pltpu.VMEM((lines, rows, cols), BF16)
+    return [DMA((7, lines)), DMA((7, lines)), small, small, small, small, large, large, large, large]
+
+
+def attend_kernel(positions, query, fresh_key, fresh_value, cache, out):
+    row = pl.program_id(0)
+    heads, head_size = query.shape[1], query.shape[2]
+    kv_cols = cache.shape[2] // 2
+    key_heads = kv_cols // head_size
+    group = heads // key_heads
+    count = cache.shape[1]
+    query_row = query[0].astype(F32)
+    inv_root = head_size ** (-0.5)
+    wide = jnp.concatenate([query_row] * key_heads, axis=1)
+    owner = lax.broadcasted_iota(jnp.int32, wide.shape, 0) // group
+    column = lax.broadcasted_iota(jnp.int32, wide.shape, 1) // head_size
+    wide = jnp.where(owner == column, wide, 0.0).astype(BF16)
+    scores = (
+        lax.dot_general(
+            wide, cache[0, :, :kv_cols], (((1,), (1,)), ((), ())), preferred_element_type=F32
+        )
+        * inv_root
+    )
+    spot = lax.broadcasted_iota(jnp.int32, scores.shape, 1)
+    scores = jnp.where(spot < positions[row], scores, -1e30)
+    fresh = jnp.sum(query_row * fresh_key[0].astype(F32), axis=-1, keepdims=True) * inv_root
+    peak = jnp.maximum(jnp.max(scores, axis=-1, keepdims=True), fresh)
+    weights = jnp.exp(scores - peak)
+    fresh_w = jnp.exp(fresh - peak)
+    total_sum = jnp.sum(weights, axis=-1, keepdims=True) + fresh_w
+    probs = (weights / total_sum).astype(BF16)
+    fresh_p = (fresh_w / total_sum).astype(BF16).astype(F32)
+    full = jnp.dot(probs, cache[0, :, kv_cols:], preferred_element_type=F32)
+    full = jnp.where(owner == column, full, 0.0)
+    result = full[:, :head_size]
+    for k in range(1, key_heads):
+        result = result + full[:, k * head_size : (k + 1) * head_size]
+    out[0] = (result + fresh_p * fresh_value[0].astype(F32)).astype(BF16)
+
+
+def attend_rows(projected, cache_rows, positions):
+    rows = projected.shape[0]
+    head_cols, kv_cols = HEADS * HD, KV * HD
+    group = HEADS // KV
+    queries = rotate(
+        projected[:, :head_cols].astype(F32).reshape(rows, HEADS, HD), positions
+    ).astype(BF16)
+    new_key = rotate(
+        projected[:, head_cols : head_cols + kv_cols].astype(F32).reshape(rows, KV, HD), positions
+    ).astype(BF16)
+    new_value = projected[:, head_cols + kv_cols :].reshape(rows, KV, HD)
+    new_key = jnp.repeat(new_key, group, axis=1)
+    new_value = jnp.repeat(new_value, group, axis=1)
+    per_row = pl.BlockSpec((1, HEADS, HD), lambda r, p: (r, 0, 0))
+    cache_spec = pl.BlockSpec((1,) + cache_rows.shape[1:], lambda r, p: (r, 0, 0))
+    result = pl.pallas_call(
+        attend_kernel,
+        grid_spec=pltpu.PrefetchScalarGridSpec(
+            num_scalar_prefetch=1,
+            grid=(rows,),
+            in_specs=[per_row, per_row, per_row, cache_spec],
+            out_specs=per_row,
+        ),
+        out_shape=jax.ShapeDtypeStruct((rows, HEADS, HD), BF16),
+        compiler_params=pltpu.CompilerParams(vmem_limit_bytes=32 * 1024 * 1024),
+    )(positions, queries, new_key, new_value, cache_rows)
+    return result.reshape(rows, head_cols)
+
+
+def score_kernel(place, rows_in, targets, weights, logits, stats, peak, total, found):
+    step = pl.program_id(0)
+    steps = pl.num_programs(0)
+    depth = rows_in.shape[2]
+    tile = jnp.dot(rows_in[0], weights[:depth, :], preferred_element_type=F32) + jnp.dot(
+        rows_in[1], weights[depth:, :], preferred_element_type=F32
+    )
+    logits[...] = tile.astype(BF16)
+
+    @pl.when(step == 0)
+    def _():
+        peak[...] = jnp.full_like(peak, -jnp.inf)
+        total[...] = jnp.zeros_like(total)
+        found[...] = jnp.zeros_like(found)
+
+    old = peak[...]
+    new = jnp.maximum(old, jnp.max(tile, axis=-1, keepdims=True))
+    total[...] = total[...] * jnp.exp(old - new) + jnp.sum(
+        jnp.exp(tile - new), axis=-1, keepdims=True
+    )
+    peak[...] = new
+    column = (
+        place[0] * tile.shape[1] * steps
+        + step * tile.shape[1]
+        + lax.broadcasted_iota(jnp.int32, tile.shape, 1)
+    )
+    found[...] += jnp.sum(jnp.where(column == targets[...], tile, 0.0), axis=-1, keepdims=True)
+
+    @pl.when(step == steps - 1)
+    def _():
+        lane = lax.broadcasted_iota(jnp.int32, stats.shape, 1)
+        stats[...] = jnp.where(
+            lane == 0, peak[...], jnp.where(lane == 1, total[...], found[...])
+        )
+
+
+def score(rows_in, targets, lm_head, tile=256):
+    _, batch_rows, depth = rows_in.shape
+    vocab_cols = lm_head.shape[1]
+    cols = vocab_cols // 2
+    member = lax.axis_index("member")
+    place = (lax.axis_index("tp") * 2 + member)[None].astype(jnp.int32)
+    steps = cols // tile
+    return pl.pallas_call(
+        score_kernel,
+        grid_spec=pltpu.PrefetchScalarGridSpec(
+            num_scalar_prefetch=1,
+            grid=(steps,),
+            in_specs=[
+                pl.BlockSpec(rows_in.shape, lambda s, p: (0, 0, 0)),
+                pl.BlockSpec((batch_rows, 1), lambda s, p: (0, 0)),
+                pl.BlockSpec((2 * depth, tile), lambda s, p: (0, lax.rem(p[0], 2) * steps + s)),
+            ],
+            out_specs=[
+                pl.BlockSpec((batch_rows, tile), lambda s, p: (0, s)),
+                pl.BlockSpec((batch_rows, 128), lambda s, p: (0, 0)),
+            ],
+            scratch_shapes=[pltpu.VMEM((batch_rows, 1), F32)] * 3,
+        ),
+        out_shape=[
+            jax.ShapeDtypeStruct((batch_rows, cols), BF16),
+            jax.ShapeDtypeStruct((batch_rows, 128), F32),
+        ],
+        compiler_params=pltpu.CompilerParams(vmem_limit_bytes=32 * 1024 * 1024),
+    )(place, rows_in, targets[:, None], lm_head)
+
+
+def close_kernel(tp_count, logits, stats, out, logprob, table, side_sem, sends, recvs):
+    tp = lax.axis_index("tp")
+    member = lax.axis_index("member")
+    cols = logits.shape[1]
+    others = []
+    for other in range(2):
+        for step in range(tp_count):
+            if other or step:
+                core = member if other == 0 else 1 - member
+                others.append({"member": core, "tp": lax.rem(tp + step, tp_count)})
+    greet(others)
+    mine = out.at[:, pl.ds(pl.multiple_of(member * cols, cols), cols)]
+    share = remote(logits, mine, sends.at[0], recvs.at[0], {"member": 1 - member})
+    local = pltpu.make_async_copy(logits, mine, side_sem)
+    local.start()
+    copies = []
+    for slot, device in enumerate(others):
+        copies.append(
+            remote(stats, table.at[slot + 1], sends.at[slot + 1], recvs.at[slot + 1], device)
+        )
+    table[0] = stats[...]
+    for copy in copies:
+        copy.wait_recv()
+    peak = jnp.max(table[:, 0, :], axis=0, keepdims=True)
+    total = jnp.sum(table[:, 1, :] * jnp.exp(table[:, 0, :] - peak), axis=0, keepdims=True)
+    found = jnp.sum(table[:, 2, :], axis=0, keepdims=True)
+    logprob[...] = found - (peak + jnp.log(total))
+    share.wait_recv()
+    local.wait()
+    share.wait_send()
+    for copy in copies:
+        copy.wait_send()
+
+
+def linked_body(
+    stream_in,
+    kv_cache,
+    lengths,
+    targets,
+    norm_gains,
+    w_qkv,
+    w_out,
+    w_gate_up,
+    w_down,
+    lm_head,
+    fast_in,
+    fast_hidden,
+    fast_out,
+):
+    tp_count = lax.axis_size("tp")
+    tp_rank = lax.axis_index("tp")
+    lines = tp_count // QUAD
+    mem_dev = fast_in.shape[0]
+    batch_rows = lengths.shape[0]
+    own_rows, width = stream_in.shape
+    all_rows = own_rows * tp_count
+    first_row = tp_rank * own_rows
+    positions = lax.dynamic_slice_in_dim(lengths, first_row % batch_rows, own_rows, 0)
+    own_member = first_row // batch_rows
+    own_scale = lax.dynamic_index_in_dim(fast_out, own_member, 0, keepdims=True)
+    own_shape = jax.ShapeDtypeStruct((own_rows, width), BF16)
+    all_shape = jax.ShapeDtypeStruct((all_rows, width), BF16)
+    own_buf = pltpu.VMEM((own_rows, width), BF16)
+
+    attn_in = call_linked(
+        functools.partial(gather_kernel, lines), 1, all_shape,
+        [own_buf] + gather_scratch(lines), (stream_in, norm_gains[0:1]),
+    )
+    projected = jnp.dot(attn_in, w_qkv, preferred_element_type=F32).astype(BF16)
+    row_major = lax.all_to_all(projected, "tp", split_axis=0, concat_axis=1, tiled=True)
+    attended = attend_rows(row_major, kv_cache, positions)
+    head_major = lax.all_to_all(attended, "tp", split_axis=1, concat_axis=0, tiled=True)
+    attn_part = jnp.dot(head_major, w_out, preferred_element_type=F32).astype(BF16)
+    middle, ffn_in = call_linked(
+        functools.partial(middle_kernel, lines), 2, [own_shape, all_shape],
+        [own_buf] + gather_scratch(lines) + sum_scratch(lines, own_rows, width),
+        (attn_part, stream_in, norm_gains[1:2]),
+    )
+    grouped = ffn_in.astype(F32).reshape(mem_dev, batch_rows, width)
+    gate_in = (grouped * fast_in[:, 0][:, None, :]).astype(BF16).reshape(all_rows, width)
+    up_in = (grouped * fast_in[:, 1][:, None, :]).astype(BF16).reshape(all_rows, width)
+    hidden_cols = w_gate_up.shape[2]
+    gate_act = (
+        jnp.dot(gate_in, w_gate_up[0], preferred_element_type=F32).reshape(
+            mem_dev, batch_rows, hidden_cols
+        )
+        * fast_hidden[:, 0][:, None, :]
+    )
+    up_act = (
+        jnp.dot(up_in, w_gate_up[1], preferred_element_type=F32).reshape(
+            mem_dev, batch_rows, hidden_cols
+        )
+        * fast_hidden[:, 1][:, None, :]
+    )
+    hidden = (
+        (jax.nn.silu(gate_act) * up_act * fast_hidden[:, 2][:, None, :])
+        .astype(BF16)
+        .reshape(all_rows, hidden_cols)
+    )
+    down_part = jnp.dot(hidden, w_down, preferred_element_type=F32).astype(BF16)
+    half = width // 2
+    mean_rows = call_linked(
+        functools.partial(final_kernel, lines), 3,
+        jax.ShapeDtypeStruct((2, batch_rows, half), BF16),
+        [
+            pltpu.VMEM((own_rows, half), F32),
+            pltpu.VMEM((own_rows, half), BF16),
+            pltpu.VMEM((own_rows, half), BF16),
+            pltpu.VMEM((own_rows, half), F32),
+            pltpu.VMEM((own_rows, half), F32),
+            pltpu.VMEM((own_rows, half), BF16),
+        ]
+        + gather_scratch(2)
+        + [DMA((3,)), DMA((3,))]
+        + sum_scratch(lines, own_rows, width),
+        (down_part, middle, own_scale, norm_gains[2:3]),
+    )
+    logits, stats = score(mean_rows, targets, lm_head)
+    stats = stats[:, :8].T
+    devices = 2 * tp_count
+    mean_logits, logprob = call_linked(
+        functools.partial(close_kernel, tp_count), 4,
+        [
+            jax.ShapeDtypeStruct((batch_rows, lm_head.shape[1]), BF16),
+            jax.ShapeDtypeStruct((1, batch_rows), F32),
+        ],
+        [pltpu.VMEM((devices, 8, batch_rows), F32), DMA, DMA((devices,)), DMA((devices,))],
+        (logits, stats),
+    )
+    return (mean_logits, logprob[0])
+
+
+def body(*args):
+    stream_in, lengths, fast_in = args[0], args[2], args[10]
+    tp_count = lax.axis_size("tp")
+    lines = tp_count // QUAD
+    whole_tiles = stream_in.shape[0] % 16 == 0
+    two_halves = lax.axis_size("member") == 2 and fast_in.shape[0] == 2
+    even_lines = tp_count % QUAD == 0 and lines % 4 == 0
+    pairs = stream_in.shape[0] * tp_count == 2 * lengths.shape[0] and lines == 4
+    if whole_tiles and two_halves and even_lines and pairs:
+        return linked_body(*args)
+    return plain_body(*args)
+
+
 def solution(mesh):
     in_specs = (
         P(("member", "tp"), None),

time: 624 us -> 226 us (0.36)
  waiting for transfers between devices: 366 us -> 15.1 us
  Pallas kernels: 0 us -> 165 us
  blocking collectives: 93 us -> 0 us
  local copies, waits for them, and re-layouts: 69.1 us -> 9.03 us
  matrix products: 55.7 us -> 20.6 us
  other arithmetic: 19.6 us -> 2.95 us
  between operations: 14.4 us -> 1.03 us
    reduce_scatter x2 -> x0, waiting for transfers between devices: 186 us -> none  [the longest x1 93.5 us: body(): lax.psum_scatter(jnp.dot(picked, w_down, preferred_element_type=jnp.float...]
    pallas_call x0 -> x6, Pallas kernels: none -> 165 us  [the longest x4 132 us: call_linked(): pl.pallas_call(kernel, out_shape=out_shape, in_specs=[VMEM] * len(args),...]
    all_gather x3 -> x0, waiting for transfers between devices: 162 us -> none  [the longest x1 61.2 us: body(): final_in = lax.all_gather(own_final, 'tp', axis=0, tiled=True)]
    pmax x1 -> x0, blocking collectives: 42 us -> none  [body(): peak = lax.pmax(local_peak, 'tp')]
    unnamed x28, local copies, waits for them, and re-layouts: 44.1 us -> 5.59 us
    psum x1 -> x0, blocking collectives: 36.5 us -> none  [body(): lax.psum((jnp.sum(jnp.exp(mean_logit - peak[:, None]), axis=-1), target_p...]
    dot_general x9 -> x5, matrix products: 55.7 us -> 20.6 us  [the longest x1 5.69 us: linked_body(): jnp.dot(up_in, w_gate_up[1], preferred_element_type=F32)]
    slice x3 -> x2, local copies, waits for them, and re-layouts: 24.8 us -> 1.79 us  [the longest x1 1.74 us: linked_body(): norm_gains[2:3]]
  transfers between devices with their start and end apart: 7 -> 2, of which waited for: 6 -> 2; matrix products, arithmetic and copies ran while one was open for 11% -> 0% of each run, Pallas kernels for 0% -> 0%
where the time goes in v1:
time: 226 us; the launch traced here: 225 us
  Pallas kernels  165 us (73%)
  matrix products  20.6 us (9%)
  waiting for transfers between devices  15.1 us (7%)
  starting transfers between devices  10.8 us (5%)
  local copies, waits for them, and re-layouts  9.03 us (4%)
  other arithmetic  2.95 us (1%)
    pallas_call x4, Pallas kernels, call_linked(): pl.pallas_call(kernel, out_shape=out_shape, in_specs=[VMEM] * len(args),...  132 us
    pallas_call x1, Pallas kernels, attend_rows(): pl.pallas_call(attend_kernel, grid_spec=pltpu.PrefetchScalarGridSpec(num_...  21.9 us
    pallas_call x1, Pallas kernels, score(): pl.pallas_call(score_kernel, grid_spec=pltpu.PrefetchScalarGridSpec(num_s...  11.1 us
    all_to_all x1, waiting for transfers between devices, linked_body(): lax.all_to_all(projected, 'tp', split_axis=0, concat_axis=1, tiled=True)  7.77 us
    all_to_all x1, waiting for transfers between devices, linked_body(): lax.all_to_all(attended, 'tp', split_axis=1, concat_axis=0, tiled=True)  7.38 us
    all_to_all x1, starting transfers between devices, linked_body(): lax.all_to_all(projected, 'tp', split_axis=0, concat_axis=1, tiled=True)  7.07 us
    dot_general x1, matrix products, linked_body(): jnp.dot(up_in, w_gate_up[1], preferred_element_type=F32)  5.69 us
    unnamed x28, local copies, waits for them, and re-layouts  5.59 us
  transfers between devices with their start and end apart: 2, of which 2 were waited for; matrix products, arithmetic and copies ran while one was open for 0% of the time, Pallas kernels for 0%

profile of v1, /device:TPU:0, one launch (start us, length us, event | category | flops | bytes accessed | tf_op | source)
XLA Modules:
  0.0 224.9 jit_solution(13737084699797604264)
XLA Ops:
  0.6 0.0 copy-start
  0.7 1.7 fusion.24
  2.4 31.3 %shard_map.140 = bf16[256,4096]{1,0:T(8,128)(2,1)} custom-call(bf16[16,4096]{1,0:T(8,128)(2,1)} %stream.3, f32[1,4096]{1,0:T(1,128)} %get-tuple-element.25.gain), custom_call_target="tpu_custom_call" | custom-call | tf_op jit(solution)/shard_map/pallas_call | solution.py:426
  33.7 0.0 copy-done
  33.7 0.0 copy-start.5
  33.7 0.0 copy-start.8
  33.7 3.6 %convolution_convert_fusion.2 = bf16[256,384]{1,0:T(8,128)(2,1)} fusion(bf16[256,4096]{1,0:T(8,128)(2,1)} %shard_map.140, bf16[4096,384]{1,0:T(8,128)(2,1)S(1)} %copy-done), kind=kOutput, calls=%fused_computation.17 | convolution fusion | flops 805404672 | bytes 5439488 | tf_op jit(solution)/shard_map/dot_general | solution.py:648
  37.3 7.1 %all-to-all-start = ((bf16[16,16,384]{2,1,0:T(8,128)(2,1)}), bf16[16,16,384]{2,1,0:T(8,128)(2,1)S(1)}, u32[]{:S(2)}, u32[]{:S(2)}) async-start(bf16[16,16,384]{2,1,0:T(8,128)(2,1)} %bitcast.1), calls=%async_computation | async-start | bytes 393216 | tf_op jit(solution)/shard_map/all_to_all | solution.py:649
  44.4 0.0 copy-done.5
  44.4 0.1 fusion.25
  44.5 0.0 copy-done.8
  44.5 0.1 fusion.23
  44.6 0.1 multiply_cosine_fusion
  44.7 7.8 %all-to-all-done = bf16[16,16,384]{2,1,0:T(8,128)(2,1)S(1)} async-done(((bf16[16,16,384]{2,1,0:T(8,128)(2,1)}), bf16[16,16,384]{2,1,0:T(8,128)(2,1)S(1)}, u32[]{:S(2)}, u32[]{:S(2)}) %all-to-all-start) | async-done | bytes 196640 | tf_op jit(solution)/shard_map/all_to_all | solution.py:649
  52.5 0.1 copy.25
  52.6 0.1 subtract_convert_fusion
  52.8 0.1 subtract_convert_fusion.1
  52.9 0.1 pad_maximum_fusion.query
  53.0 0.1 pad_maximum_fusion.1
  53.2 0.0 copy-start.7
  53.2 0.0 copy-start.6
  53.2 0.0 copy-start.4
  53.2 21.9 %shard_map.141 = bf16[16,32,128]{2,1,0:T(8,128)(2,1)S(1)} custom-call(s32[16]{0:T(128)S(1)} %get-tuple-element.15.positions, bf16[16,32,128]{2,1,0:T(8,128)(2,1)S(1)} %pad_maximum_fusion.query, bf16[16,32,128]{2,1,0:T(8,128)(2,1)S(1)} %bitcast.66, bf16[16,32,128]{2,1,0:T(8,128)(2,1)S(1)} %bitcast.67, bf16[16,512,2048]{2,1,0:T(8,128)(2,1)} %cache.1), custom_call_target="tpu_custom_call" | custom-call | tf_op jit(solution)/shard_map/pallas_call | solution.py:499
  75.2 0.7 copy.19
  75.9 3.7 %all-to-all-start.1 = ((bf16[16,16,256]{2,0,1:T(8,128)(2,1)}), bf16[16,16,256]{2,0,1:T(8,128)(2,1)S(1)}, u32[]{:S(2)}, u32[]{:S(2)}) async-start(bf16[16,16,256]{2,0,1:T(8,128)(2,1)} %copy.19), calls=%async_computation.1 | async-start | bytes 262144 | tf_op jit(solution)/shard_map/all_to_all | solution.py:651
  79.6 0.1 copy_bitcast_fusion
  79.6 0.0 copy-done.7
  79.7 0.1 copy.20.targets
  79.8 0.0 copy-done.6
  79.8 7.4 %all-to-all-done.1 = bf16[16,16,256]{2,0,1:T(8,128)(2,1)S(1)} async-done(((bf16[16,16,256]{2,0,1:T(8,128)(2,1)}), bf16[16,16,256]{2,0,1:T(8,128)(2,1)S(1)}, u32[]{:S(2)}, u32[]{:S(2)}) %all-to-all-start.1) | async-done | bytes 131104 | tf_op jit(solution)/shard_map/all_to_all | solution.py:651
  87.2 0.0 copy-done.4
  87.2 2.1 convolution_convert_fusion.1.part
  89.2 45.0 %shard_map.142 = (bf16[16,4096]{1,0:T(8,128)(2,1)}, bf16[256,4096]{1,0:T(8,128)(2,1)}) custom-call(bf16[256,4096]{1,0:T(8,128)(2,1)} %convolution_convert_fusion.1.part, bf16[16,4096]{1,0:T(8,128)(2,1)} %stream.3, f32[1,4096]{1,0:T(1,128)} %get-tuple-element.26.gain), custom_call_target="tpu_custom_call" | custom-call | tf_op jit(solution)/shard_map/pallas_call | solution.py:426
  134.2 2.3 %fusion.6 = (bf16[256,4096]{1,0:T(8,128)(2,1)S(1)}, bf16[256,4096]{1,0:T(8,128)(2,1)S(1)}) fusion(bf16[256,4096]{1,0:T(8,128)(2,1)} %get-tuple-element.8, f32[2,4096]{1,0:T(2,128)S(1)} %get-tuple-element.35, f32[2,4096]{1,0:T(2,128)S(1)} %get-tuple-element.34), kind=kLoop, calls=%fused_computation.10 | loop fusion | flops 5242880 | bytes 6356992 | tf_op jit(solution)/shard_map/convert_element_type | solution.py:659
  136.5 0.0 slice-start
  136.5 5.6 %fusion.8 = f32[2,128,896]{2,1,0:T(8,128)S(1)} fusion(bf16[2,128,4096]{2,1,0:T(8,128)(2,1)S(1)} %bitcast.70, bf16[2,4096,896]{2,1,0:T(8,128)(2,1)} %param.20, f32[2,896]{1,0:T(2,128)S(1)} %get-tuple-element.30), kind=kOutput, calls=%fused_computation.12 | convolution fusion | flops 1879277568 | bytes 10361856 | tf_op jit(solution)/shard_map/dot_general | solution.py:663
  142.1 0.0 slice-start.1
  142.1 5.7 %fusion.20 = bf16[2,128,896]{2,1,0:T(8,128)(2,1)S(1)} fusion(bf16[2,128,4096]{2,1,0:T(8,128)(2,1)S(1)} %bitcast.69, bf16[2,4096,896]{2,1,0:T(8,128)(2,1)} %param.20, f32[2,128,896]{2,1,0:T(8,128)S(1)} %fusion.8, f32[2,896]{1,0:T(2,128)S(1)} %get-tuple-element.31, f32[2,896]{1,0:T(2,128)S(1)} %get-tuple-element.29), kind=kOutput, calls=%fused_computation.16 | convolution fusion | flops 1880883200 | bytes 10827776 | tf_op jit(solution)/shard_map/dot_general | solution.py:669
  147.8 0.0 slice-done
  147.8 0.0 slice-done.1
  147.8 3.8 %convolution_convert_fusion.part = bf16[256,4096]{1,0:T(8,128)(2,1)} fusion(bf16[256,896]{1,0:T(8,128)(2,1)S(1)} %bitcast.81, bf16[896,4096]{1,0:T(8,128)(2,1)S(1)} %bitcast.79), kind=kOutput, calls=%fused_computation.8 | convolution fusion | flops 1880096768 | bytes 9895936 | tf_op jit(solution)/shard_map/dot_general | solution.py:679
  151.6 44.7 %shard_map.143.rows_in = bf16[2,128,2048]{2,1,0:T(8,128)(2,1)} custom-call(bf16[256,4096]{1,0:T(8,128)(2,1)} %convolution_convert_fusion.part, bf16[16,4096]{1,0:T(8,128)(2,1)} %get-tuple-element.9.middle, f32[1,4096]{1,0:T(1,128)} %get-tuple-element.36.scale, f32[1,4096]{1,0:T(1,128)} %get-tuple-element.24.gain), custom_call_target="tpu_custom_call" | custom-call | tf_op jit(solution)/shard_map/pallas_call | solution.py:426
  196.3 0.0 copy-start.2
  196.3 1.2 copy-done.2
  197.5 0.0 copy-start.1
  197.5 11.1 %shard_map.144 = (bf16[128,2048]{1,0:T(8,128)(2,1)S(1)}, f32[128,128]{1,0:T(8,128)S(1)}) custom-call(s32[1]{0:T(128)} %bitcast.place, bf16[2,128,2048]{2,1,0:T(8,128)(2,1)S(1)} %copy-done.2, s32[128,1]{1,0:T(8,128)S(1)} %copy.20.targets, bf16[4096,4096]{1,0:T(8,128)(2,1)} %weights.1), custom_call_target="tpu_custom_call" | custom-call | tf_op jit(solution)/shard_map/pallas_call | solution.py:556
  208.6 0.0 copy-start.3
  208.6 0.8 copy-done.3
  209.4 0.1 copy.21
  209.5 0.6 slice_bitcast_fusion.4.stats
  210.1 11.4 %shard_map.145 = (bf16[128,4096]{1,0:T(8,128)(2,1)}, f32[1,128]{1,0:T(1,128)}) custom-call(bf16[128,2048]{1,0:T(8,128)(2,1)} %copy-done.3, f32[8,128]{1,0:T(8,128)} %slice_bitcast_fusion.4.stats), custom_call_target="tpu_custom_call" | custom-call | tf_op jit(solution)/shard_map/pallas_call | solution.py:426
  221.5 2.3 %copy.32 = bf16[128,4096]{1,0:T(8,128)(2,1)} copy(bf16[128,4096]{1,0:T(8,128)(2,1)} %get-tuple-element.39) | data formatting | bytes 2097152
  223.7 1.1 copy.33
  224.9 0.0 copy-done.1
  (11 shorter events, 0.2 us)
Async XLA Ops:
  0.6 33.1 %copy-start = (bf16[4096,384]{1,0:T(8,128)(2,1)S(1)}, bf16[4096,384]{1,0:T(8,128)(2,1)}, u32[]{:S(2)}) copy-start(bf16[4096,384]{1,0:T(8,128)(2,1)} %param.18) | copy-start | bytes 9437188
  33.7 10.7 %copy-start.5 = (f32[2,2,4096]{2,1,0:T(2,128)S(1)}, f32[2,2,4096]{2,1,0:T(2,128)}, u32[]{:S(2)}) copy-start(f32[2,2,4096]{2,1,0:T(2,128)} %param.23) | copy-start | bytes 196612
  33.7 10.8 %copy-start.8 = (s32[128]{0:T(128)S(1)}, s32[128]{0:T(128)}, u32[]{:S(2)}) copy-start(s32[128]{0:T(128)} %param.15) | copy-start | bytes 1540
  37.3 15.2 %all-to-all-start = ((bf16[16,16,384]{2,1,0:T(8,128)(2,1)}), bf16[16,16,384]{2,1,0:T(8,128)(2,1)S(1)}, u32[]{:S(2)}, u32[]{:S(2)}) async-start(bf16[16,16,384]{2,1,0:T(8,128)(2,1)} %bitcast.1), calls=%async_computation | async-start | bytes 393216 | tf_op jit(solution)/shard_map/all_to_all | solution.py:649
  53.2 26.5 %copy-start.7 = (s32[128]{0:T(128)S(1)}, s32[128]{0:T(128)}, u32[]{:S(2)}) copy-start(s32[128]{0:T(128)} %param.16) | copy-start | bytes 1540
  53.2 26.6 %copy-start.6 = (f32[2,3,896]{2,0,1:T(2,128)S(1)}, f32[2,3,896]{2,0,1:T(2,128)}, u32[]{:S(2)}) copy-start(f32[2,3,896]{2,0,1:T(2,128)} %param.24) | copy-start | bytes 64516
  53.2 34.0 %copy-start.4 = (bf16[256,4096]{1,0:T(8,128)(2,1)S(1)}, bf16[256,4096]{1,0:T(8,128)(2,1)}, u32[]{:S(2)}) copy-start(bf16[256,4096]{1,0:T(8,128)(2,1)} %param.19) | copy-start | bytes 6291460
  75.9 11.3 %all-to-all-start.1 = ((bf16[16,16,256]{2,0,1:T(8,128)(2,1)}), bf16[16,16,256]{2,0,1:T(8,128)(2,1)S(1)}, u32[]{:S(2)}, u32[]{:S(2)}) async-start(bf16[16,16,256]{2,0,1:T(8,128)(2,1)} %copy.19), calls=%async_computation.1 | async-start | bytes 262144 | tf_op jit(solution)/shard_map/all_to_all | solution.py:651
  136.5 11.3 %slice-start = ((s8[7340032]{0:T(1024)(128)(4,1)}), s8[3145728]{0:T(1024)(128)(4,1)S(1)}, s32[]{:S(2)}) async-start(s8[7340032]{0:T(1024)(128)(4,1)} %bitcast.78), calls=%async_computation.2 | async-start | bytes 6291456
  142.1 5.7 %slice-start.1 = ((s8[7340032]{0:T(1024)(128)(4,1)}), s8[4194304]{0:T(1024)(128)(4,1)S(1)}, s32[]{:S(2)}) async-start(s8[7340032]{0:T(1024)(128)(4,1)} %bitcast.78), calls=%async_computation.3 | async-start | bytes 8388608
  196.3 1.2 copy-start.2
  197.5 27.3 %copy-start.1 = (bf16[4096,384]{1,0:T(8,128)(2,1)S(1)}, bf16[4096,384]{1,0:T(8,128)(2,1)}, u32[]{:S(2)}) copy-start(bf16[4096,384]{1,0:T(8,128)(2,1)} %param.18) | copy-start | bytes 9437188
  208.6 0.8 copy-start.3

commit v2 on v1

--- a/solution.py
+++ b/solution.py
@@ -359,45 +359,104 @@
     )
 
 
-def middle_kernel(
-    lines, part, stream, gain, middle, out, own, local_sem, sends, recvs, sum_sends, sum_recvs, *bufs
+def tail_kernel(
+    lines, heads_in, w_out, stream, gains, fast_in, fast_hidden, scale, targets, w_gate_up, w_down, lm_head,
+    out, logprob,
+    part, middle, ffn_in, acts, hidden, gate_up, down, words, own, half_own, away, from_core,
+    pair, from_pair, mean, rows_in, stats, table,
+    load_sems, tile_sends, tile_recvs, stat_sends, stat_recvs, side_sends, side_recvs,
+    local_sem, sends, recvs, last_sem, last_sends, last_recvs, *sums
 ):
     place = Place(lines)
-    greet(near(place))
-    total = sum_rows(place, part, (sum_sends, sum_recvs), bufs)
+    tp_count = lines * QUAD
+    member = place.member
+    cols = words.shape[1]
+    other = {"member": 1 - member}
+    loads = [
+        pltpu.make_async_copy(w_gate_up, gate_up, load_sems.at[0]),
+        pltpu.make_async_copy(w_down, down, load_sems.at[1]),
+        pltpu.make_async_copy(
+            lm_head.at[:, pl.ds(pl.multiple_of(member * cols, cols), cols)], words, load_sems.at[2]
+        ),
+    ]
+    for load in loads:
+        load.start()
+    others = []
+    for core in (member, 1 - member):
+        for step in range(tp_count):
+            if others or step:
+                others.append({"member": core, "tp": lax.rem(place.tp + step, tp_count)})
+    greet(others)
+    wide = 512
+
+    @pl.loop(0, part.shape[1] // wide)
+    def _(i):
+        span = pl.ds(pl.multiple_of(i * wide, wide), wide)
+        part[:, span] = jnp.dot(
+            heads_in[...], w_out[:, span], preferred_element_type=F32
+        ).astype(BF16)
+
+    count = len(sums) // 2
+    total = sum_rows(place, part, sums[:2], sums[2:count])
     middle[...] = (stream[...].astype(F32) + total).astype(BF16)
-    own[...] = norm_rows(middle[...].astype(F32), gain[...]).astype(BF16)
+    own[...] = norm_rows(middle[...].astype(F32), gains[1][:1]).astype(BF16)
     gather_rows(
-        place, own, out, (local_sem, sends, recvs), list(range(lines)),
+        place, own, ffn_in, (local_sem, sends, recvs), list(range(lines)),
         lambda step, quad: place.line_at(step) * QUAD + quad,
     )
-
-
-def final_kernel(
-    lines, part, middle, scale, gain, out,
-    own, away, from_core, pair, from_pair, mean,
-    local_sem, sends, recvs, side_sends, side_recvs, sum_sends, sum_recvs, *bufs
-):
-    place = Place(lines)
-    other = {"member": 1 - place.member}
-    greet(near(place) + [other])
-    total = sum_rows(place, part, (sum_sends, sum_recvs), bufs)
+    loads[0].wait()
+    members = fast_in.shape[0]
+    batch_rows = ffn_in.shape[0] // members
+    acts[...] = jnp.zeros_like(acts)
+
+    @pl.loop(0, ffn_in.shape[1] // wide)
+    def _(i):
+        span = pl.ds(pl.multiple_of(i * wide, wide), wide)
+        values = ffn_in[:, span].astype(F32)
+        for j in range(2):
+            scaled = jnp.concatenate(
+                [
+                    values[m * batch_rows : (m + 1) * batch_rows] * fast_in[m, j, :, span][:1]
+                    for m in range(members)
+                ],
+                axis=0,
+            ).astype(BF16)
+            acts[j] += jnp.dot(scaled, gate_up[j, span, :], preferred_element_type=F32)
+
+    for m in range(members):
+        rows = slice(m * batch_rows, (m + 1) * batch_rows)
+        gate = acts[0, rows, :] * fast_hidden[m, 0][:1]
+        hidden[rows, :] = (
+            gate / (1.0 + jnp.exp(-gate))
+            * (acts[1, rows, :] * fast_hidden[m, 1][:1])
+            * fast_hidden[m, 2][:1]
+        ).astype(BF16)
+    loads[1].wait()
+
+    @pl.loop(0, part.shape[1] // wide)
+    def _(i):
+        span = pl.ds(pl.multiple_of(i * wide, wide), wide)
+        part[:, span] = jnp.dot(
+            hidden[...], down[:, span], preferred_element_type=F32
+        ).astype(BF16)
+
+    total = sum_rows(place, part, sums[count : count + 2], sums[count + 2 :])
     layer_out = (middle[...].astype(F32) + total * scale[...]).astype(BF16)
-    normed = norm_rows(layer_out.astype(F32), gain[...]).astype(BF16)
+    normed = norm_rows(layer_out.astype(F32), gains[2][:1]).astype(BF16)
     half = mean.shape[1]
-    first = place.member == 0
-    low, high = normed[:, :half], normed[:, half:]
-    own[...] = jnp.where(first, low.astype(F32), high.astype(F32))
-    away[...] = jnp.where(first, high.astype(F32), low.astype(F32)).astype(BF16)
+    first = member == 0
+    low, high = normed[:, :half].astype(F32), normed[:, half:].astype(F32)
+    half_own[...] = jnp.where(first, low, high)
+    away[...] = jnp.where(first, high, low).astype(BF16)
     core = remote(away, from_core, side_sends.at[0], side_recvs.at[0], other)
     core.wait_recv()
-    own[...] = own[...] + from_core[...].astype(F32)
-    pair[...] = own[...]
+    half_own[...] = half_own[...] + from_core[...].astype(F32)
+    pair[...] = half_own[...]
     twin = remote(
         pair, from_pair, side_sends.at[1], side_recvs.at[1], place.to_line(lines // 2)
     )
     twin.wait_recv()
-    mean[...] = ((own[...] + from_pair[...]) * 0.25).astype(BF16)
+    mean[...] = ((half_own[...] + from_pair[...]) * 0.25).astype(BF16)
     turn = 1 - 2 * lax.rem(place.line, 2)
 
     class Pairwise:
@@ -407,31 +466,78 @@
     near_line.quad, near_line.quad_x, near_line.quad_y = place.quad, place.quad_x, place.quad_y
     near_line.to_x, near_line.to_y = place.to_x, place.to_y
     near_line.to_line = lambda step: {"tp": (place.line + turn) * QUAD + place.quad}
-    mine = out.at[place.member]
+    mine = rows_in.at[member]
     gather_rows(
-        near_line, mean, mine, (local_sem, sends, recvs), [0, 1],
+        near_line, mean, mine, (last_sem, last_sends, last_recvs), [0, 1],
         lambda step, quad: lax.rem(place.line + abs(step), 2) * QUAD + quad,
     )
     share = remote(mine, mine, side_sends.at[2], side_recvs.at[2], other)
+    loads[2].wait()
     share.wait_recv()
-    for copy in (core, twin, share):
+    tile_width = cols // tile_sends.shape[0]
+    batch = rows_in.shape[1]
+    peak = jnp.full((batch, 1), -jnp.inf, F32)
+    amount = jnp.zeros((batch, 1), F32)
+    found = jnp.zeros((batch, 1), F32)
+    tiles = []
+    for i in range(tile_sends.shape[0]):
+        span = pl.ds(i * tile_width, tile_width)
+        tile = jnp.dot(rows_in[0], words[:half, span], preferred_element_type=F32) + jnp.dot(
+            rows_in[1], words[half:, span], preferred_element_type=F32
+        )
+        into = out.at[:, pl.ds(pl.multiple_of(member * cols + i * tile_width, tile_width), tile_width)]
+        into[...] = tile.astype(BF16)
+        tiles.append(remote(into, into, tile_sends.at[i], tile_recvs.at[i], other))
+        new = jnp.maximum(peak, jnp.max(tile, axis=-1, keepdims=True))
+        amount = amount * jnp.exp(peak - new) + jnp.sum(
+            jnp.exp(tile - new), axis=-1, keepdims=True
+        )
+        peak = new
+        column = (
+            (place.tp * 2 + member) * cols
+            + i * tile_width
+            + lax.broadcasted_iota(jnp.int32, tile.shape, 1)
+        )
+        found = found + jnp.sum(
+            jnp.where(column == targets[...], tile, 0.0), axis=-1, keepdims=True
+        )
+    lane = lax.broadcasted_iota(jnp.int32, (batch, 128), 1)
+    block = jnp.where(lane == 0, peak, jnp.where(lane == 1, amount, found))
+    stats[...] = jnp.transpose(block)[:8, :]
+    copies = []
+    for slot, device in enumerate(others):
+        copies.append(
+            remote(stats, table.at[slot + 1], stat_sends.at[slot], stat_recvs.at[slot], device)
+        )
+    table[0] = stats[...]
+    for copy in copies:
+        copy.wait_recv()
+    top = jnp.max(table[:, 0, :], axis=0, keepdims=True)
+    amount = jnp.sum(table[:, 1, :] * jnp.exp(table[:, 0, :] - top), axis=0, keepdims=True)
+    found = jnp.sum(table[:, 2, :], axis=0, keepdims=True)
+    logprob[...] = found - (top + jnp.log(amount))
+    for copy in tiles:
+        copy.wait_recv()
+    for copy in [core, twin, share] + tiles + copies:
         copy.wait_send()
 
 
 VMEM = pl.BlockSpec(memory_space=pltpu.VMEM)
-VMEM_BYTES = 60 * 1024 * 1024
-
-
-def call_linked(kernel, number, out_shape, scratch, args):
+ANY = pl.BlockSpec(memory_space=pl.ANY)
+MIB = 1024 * 1024
+
+
+def call_linked(kernel, number, out_shape, scratch, args, mib, far=0):
     return pl.pallas_call(
         kernel,
         out_shape=out_shape,
-        in_specs=[VMEM] * len(args),
+        in_specs=[VMEM] * (len(args) - far) + [ANY] * far,
         out_specs=jax.tree.map(lambda _: VMEM, out_shape),
         scratch_shapes=scratch,
         compiler_params=pltpu.CompilerParams(
-            collective_id=number, has_side_effects=True, vmem_limit_bytes=VMEM_BYTES
+            collective_id=number, has_side_effects=True, vmem_limit_bytes=mib * MIB
         ),
+        cost_estimate=pl.CostEstimate(flops=0, bytes_accessed=64 * MIB, transcendentals=0),
     )(*args)
 
 
@@ -510,105 +616,8 @@
     return result.reshape(rows, head_cols)
 
 
-def score_kernel(place, rows_in, targets, weights, logits, stats, peak, total, found):
-    step = pl.program_id(0)
-    steps = pl.num_programs(0)
-    depth = rows_in.shape[2]
-    tile = jnp.dot(rows_in[0], weights[:depth, :], preferred_element_type=F32) + jnp.dot(
-        rows_in[1], weights[depth:, :], preferred_element_type=F32
-    )
-    logits[...] = tile.astype(BF16)
-
-    @pl.when(step == 0)
-    def _():
-        peak[...] = jnp.full_like(peak, -jnp.inf)
-        total[...] = jnp.zeros_like(total)
-        found[...] = jnp.zeros_like(found)
-
-    old = peak[...]
-    new = jnp.maximum(old, jnp.max(tile, axis=-1, keepdims=True))
-    total[...] = total[...] * jnp.exp(old - new) + jnp.sum(
-        jnp.exp(tile - new), axis=-1, keepdims=True
-    )
-    peak[...] = new
-    column = (
-        place[0] * tile.shape[1] * steps
-        + step * tile.shape[1]
-        + lax.broadcasted_iota(jnp.int32, tile.shape, 1)
-    )
-    found[...] += jnp.sum(jnp.where(column == targets[...], tile, 0.0), axis=-1, keepdims=True)
-
-    @pl.when(step == steps - 1)
-    def _():
-        lane = lax.broadcasted_iota(jnp.int32, stats.shape, 1)
-        stats[...] = jnp.where(
-            lane == 0, peak[...], jnp.where(lane == 1, total[...], found[...])
-        )
-
-
-def score(rows_in, targets, lm_head, tile=256):
-    _, batch_rows, depth = rows_in.shape
-    vocab_cols = lm_head.shape[1]
-    cols = vocab_cols // 2
-    member = lax.axis_index("member")
-    place = (lax.axis_index("tp") * 2 + member)[None].astype(jnp.int32)
-    steps = cols // tile
-    return pl.pallas_call(
-        score_kernel,
-        grid_spec=pltpu.PrefetchScalarGridSpec(
-            num_scalar_prefetch=1,
-            grid=(steps,),
-            in_specs=[
-                pl.BlockSpec(rows_in.shape, lambda s, p: (0, 0, 0)),
-                pl.BlockSpec((batch_rows, 1), lambda s, p: (0, 0)),
-                pl.BlockSpec((2 * depth, tile), lambda s, p: (0, lax.rem(p[0], 2) * steps + s)),
-            ],
-            out_specs=[
-                pl.BlockSpec((batch_rows, tile), lambda s, p: (0, s)),
-                pl.BlockSpec((batch_rows, 128), lambda s, p: (0, 0)),
-            ],
-            scratch_shapes=[pltpu.VMEM((batch_rows, 1), F32)] * 3,
-        ),
-        out_shape=[
-            jax.ShapeDtypeStruct((batch_rows, cols), BF16),
-            jax.ShapeDtypeStruct((batch_rows, 128), F32),
-        ],
-        compiler_params=pltpu.CompilerParams(vmem_limit_bytes=32 * 1024 * 1024),
-    )(place, rows_in, targets[:, None], lm_head)
-
-
-def close_kernel(tp_count, logits, stats, out, logprob, table, side_sem, sends, recvs):
-    tp = lax.axis_index("tp")
-    member = lax.axis_index("member")
-    cols = logits.shape[1]
-    others = []
-    for other in range(2):
-        for step in range(tp_count):
-            if other or step:
-                core = member if other == 0 else 1 - member
-                others.append({"member": core, "tp": lax.rem(tp + step, tp_count)})
-    greet(others)
-    mine = out.at[:, pl.ds(pl.multiple_of(member * cols, cols), cols)]
-    share = remote(logits, mine, sends.at[0], recvs.at[0], {"member": 1 - member})
-    local = pltpu.make_async_copy(logits, mine, side_sem)
-    local.start()
-    copies = []
-    for slot, device in enumerate(others):
-        copies.append(
-            remote(stats, table.at[slot + 1], sends.at[slot + 1], recvs.at[slot + 1], device)
-        )
-    table[0] = stats[...]
-    for copy in copies:
-        copy.wait_recv()
-    peak = jnp.max(table[:, 0, :], axis=0, keepdims=True)
-    total = jnp.sum(table[:, 1, :] * jnp.exp(table[:, 0, :] - peak), axis=0, keepdims=True)
-    found = jnp.sum(table[:, 2, :], axis=0, keepdims=True)
-    logprob[...] = found - (peak + jnp.log(total))
-    share.wait_recv()
-    local.wait()
-    share.wait_send()
-    for copy in copies:
-        copy.wait_send()
+def whole_tiles(rows):
+    return jnp.broadcast_to(rows[..., None, :], rows.shape[:-1] + (8, rows.shape[-1]))
 
 
 def linked_body(
@@ -629,7 +638,6 @@
     tp_count = lax.axis_size("tp")
     tp_rank = lax.axis_index("tp")
     lines = tp_count // QUAD
-    mem_dev = fast_in.shape[0]
     batch_rows = lengths.shape[0]
     own_rows, width = stream_in.shape
     all_rows = own_rows * tp_count
@@ -637,74 +645,58 @@
     positions = lax.dynamic_slice_in_dim(lengths, first_row % batch_rows, own_rows, 0)
     own_member = first_row // batch_rows
     own_scale = lax.dynamic_index_in_dim(fast_out, own_member, 0, keepdims=True)
-    own_shape = jax.ShapeDtypeStruct((own_rows, width), BF16)
     all_shape = jax.ShapeDtypeStruct((all_rows, width), BF16)
     own_buf = pltpu.VMEM((own_rows, width), BF16)
 
     attn_in = call_linked(
         functools.partial(gather_kernel, lines), 1, all_shape,
-        [own_buf] + gather_scratch(lines), (stream_in, norm_gains[0:1]),
+        [own_buf] + gather_scratch(lines), (stream_in, norm_gains[0:1]), 16,
     )
     projected = jnp.dot(attn_in, w_qkv, preferred_element_type=F32).astype(BF16)
     row_major = lax.all_to_all(projected, "tp", split_axis=0, concat_axis=1, tiled=True)
     attended = attend_rows(row_major, kv_cache, positions)
     head_major = lax.all_to_all(attended, "tp", split_axis=1, concat_axis=0, tiled=True)
-    attn_part = jnp.dot(head_major, w_out, preferred_element_type=F32).astype(BF16)
-    middle, ffn_in = call_linked(
-        functools.partial(middle_kernel, lines), 2, [own_shape, all_shape],
-        [own_buf] + gather_scratch(lines) + sum_scratch(lines, own_rows, width),
-        (attn_part, stream_in, norm_gains[1:2]),
-    )
-    grouped = ffn_in.astype(F32).reshape(mem_dev, batch_rows, width)
-    gate_in = (grouped * fast_in[:, 0][:, None, :]).astype(BF16).reshape(all_rows, width)
-    up_in = (grouped * fast_in[:, 1][:, None, :]).astype(BF16).reshape(all_rows, width)
-    hidden_cols = w_gate_up.shape[2]
-    gate_act = (
-        jnp.dot(gate_in, w_gate_up[0], preferred_element_type=F32).reshape(
-            mem_dev, batch_rows, hidden_cols
-        )
-        * fast_hidden[:, 0][:, None, :]
-    )
-    up_act = (
-        jnp.dot(up_in, w_gate_up[1], preferred_element_type=F32).reshape(
-            mem_dev, batch_rows, hidden_cols
-        )
-        * fast_hidden[:, 1][:, None, :]
-    )
-    hidden = (
-        (jax.nn.silu(gate_act) * up_act * fast_hidden[:, 2][:, None, :])
-        .astype(BF16)
-        .reshape(all_rows, hidden_cols)
-    )
-    down_part = jnp.dot(hidden, w_down, preferred_element_type=F32).astype(BF16)
     half = width // 2
-    mean_rows = call_linked(
-        functools.partial(final_kernel, lines), 3,
-        jax.ShapeDtypeStruct((2, batch_rows, half), BF16),
+    devices = 2 * tp_count
+    vocab_cols = lm_head.shape[1]
+    tiles = 4
+    mean_logits, logprob = call_linked(
+        functools.partial(tail_kernel, lines), 2,
         [
+            jax.ShapeDtypeStruct((batch_rows, vocab_cols), BF16),
+            jax.ShapeDtypeStruct((1, batch_rows), F32),
+        ],
+        [
+            pltpu.VMEM((all_rows, width), BF16),
+            own_buf,
+            pltpu.VMEM((all_rows, width), BF16),
+            pltpu.VMEM((2, all_rows, w_gate_up.shape[2]), F32),
+            pltpu.VMEM((all_rows, w_gate_up.shape[2]), BF16),
+            pltpu.VMEM(w_gate_up.shape, BF16),
+            pltpu.VMEM(w_down.shape, BF16),
+            pltpu.VMEM((width, vocab_cols // 2), BF16),
+            own_buf,
             pltpu.VMEM((own_rows, half), F32),
             pltpu.VMEM((own_rows, half), BF16),
             pltpu.VMEM((own_rows, half), BF16),
             pltpu.VMEM((own_rows, half), F32),
             pltpu.VMEM((own_rows, half), F32),
             pltpu.VMEM((own_rows, half), BF16),
+            pltpu.VMEM((2, batch_rows, half), BF16),
+            pltpu.VMEM((8, batch_rows), F32),
+            pltpu.VMEM((devices, 8, batch_rows), F32),
+            DMA((3,)), DMA((tiles,)), DMA((tiles,)), DMA((devices,)), DMA((devices,)), DMA((3,)), DMA((3,)),
         ]
+        + gather_scratch(lines)
         + gather_scratch(2)
-        + [DMA((3,)), DMA((3,))]
+        + sum_scratch(lines, own_rows, width)
         + sum_scratch(lines, own_rows, width),
-        (down_part, middle, own_scale, norm_gains[2:3]),
-    )
-    logits, stats = score(mean_rows, targets, lm_head)
-    stats = stats[:, :8].T
-    devices = 2 * tp_count
-    mean_logits, logprob = call_linked(
-        functools.partial(close_kernel, tp_count), 4,
-        [
-            jax.ShapeDtypeStruct((batch_rows, lm_head.shape[1]), BF16),
-            jax.ShapeDtypeStruct((1, batch_rows), F32),
-        ],
-        [pltpu.VMEM((devices, 8, batch_rows), F32), DMA, DMA((devices,)), DMA((devices,))],
-        (logits, stats),
+        (
+            head_major, w_out, stream_in, whole_tiles(norm_gains), whole_tiles(fast_in),
+            whole_tiles(fast_hidden), own_scale, targets[:, None],
+            w_gate_up, w_down, lm_head,
+        ),
+        58, 3,
     )
     return (mean_logits, logprob[0])
 
@@ -713,11 +705,11 @@
     stream_in, lengths, fast_in = args[0], args[2], args[10]
     tp_count = lax.axis_size("tp")
     lines = tp_count // QUAD
-    whole_tiles = stream_in.shape[0] % 16 == 0
+    full_rows = stream_in.shape[0] % 16 == 0
     two_halves = lax.axis_size("member") == 2 and fast_in.shape[0] == 2
     even_lines = tp_count % QUAD == 0 and lines % 4 == 0
     pairs = stream_in.shape[0] * tp_count == 2 * lengths.shape[0] and lines == 4
-    if whole_tiles and two_halves and even_lines and pairs:
+    if full_rows and two_halves and even_lines and pairs:
         return linked_body(*args)
     return plain_body(*args)
 

time: 226 us -> 209 us (0.925)
  matrix products: 20.6 us -> 1.97 us
  Pallas kernels: 165 us -> 170 us
  other arithmetic: 2.95 us -> 0.67 us
    dot_general x4 -> x0, matrix products: 17.1 us -> none  [the longest x1 5.69 us: linked_body(): jnp.dot(up_in, w_gate_up[1], preferred_element_type=F32)]
    pallas_call x5 -> x2, Pallas kernels: 143 us -> 148 us  [call_linked(): pl.pallas_call(kernel, out_shape=out_shape, in_specs=[VMEM] * (len(args)...]
    broadcast_in_dim x1 -> x4, local copies, waits for them, and re-layouts: 0.11 us -> 3.03 us  [the longest x3 2.29 us: whole_tiles(): jnp.broadcast_to(rows[..., None, :], rows.shape[:-1] + (8, rows.shape[-1]))]
    convert_element_type x1 -> x0, other arithmetic: 2.29 us -> none  [linked_body(): (grouped * fast_in[:, 0][:, None, :]).astype(BF16).reshape(all_rows, width)]
    unnamed x28 -> x26, local copies, waits for them, and re-layouts: 5.59 us -> 4.5 us
  transfers between devices with their start and end apart: 2 -> 2, of which waited for: 2 -> 2; matrix products, arithmetic and copies ran while one was open for 0% -> 1% of each run, Pallas kernels for 0% -> 0%
where the time goes in v2:
time: 209 us; the launch traced here: 208 us
  Pallas kernels  170 us (81%)
  waiting for transfers between devices  14.2 us (7%)
  starting transfers between devices  10.6 us (5%)
  local copies, waits for them, and re-layouts  10 us (5%)
    pallas_call x2, Pallas kernels, call_linked(): pl.pallas_call(kernel, out_shape=out_shape, in_specs=[VMEM] * (len(args)...  148 us
    pallas_call x1, Pallas kernels, attend_rows(): pl.pallas_call(attend_kernel, grid_spec=pltpu.PrefetchScalarGridSpec(num_...  21.8 us
    all_to_all x1, waiting for transfers between devices, linked_body(): lax.all_to_all(attended, 'tp', split_axis=1, concat_axis=0, tiled=True)  7.13 us
    all_to_all x1, starting transfers between devices, linked_body(): lax.all_to_all(projected, 'tp', split_axis=0, concat_axis=1, tiled=True)  7.07 us
    all_to_all x1, waiting for transfers between devices, linked_body(): lax.all_to_all(projected, 'tp', split_axis=0, concat_axis=1, tiled=True)  7.07 us
    unnamed x26, local copies, waits for them, and re-layouts  4.5 us
  transfers between devices with their start and end apart: 2, of which 2 were waited for; matrix products, arithmetic and copies ran while one was open for 1% of the time, Pallas kernels for 0%

profile of v2, /device:TPU:0, one launch (start us, length us, event | category | flops | bytes accessed | tf_op | source)
XLA Modules:
  0.0 208.0 jit_solution(6020488717692503884)
XLA Ops:
  0.6 0.0 copy-start
  0.6 1.0 slice.24.gain
  1.7 0.0 copy-start.2
  1.7 0.9 copy-done.2
  2.6 29.0 %shard_map.140 = bf16[256,4096]{1,0:T(8,128)(2,1)S(1)} custom-call(bf16[16,4096]{1,0:T(8,128)(2,1)S(1)} %copy-done.2, f32[1,4096]{1,0:T(1,128)S(1)} %slice.24.gain), custom_call_target="tpu_custom_call" | custom-call | bytes 67108864 | tf_op jit(solution)/shard_map/pallas_call | solution.py:531
  31.6 0.0 copy-done
  31.6 0.0 copy-start.6
  31.6 0.0 copy-start.8
  31.6 0.0 copy-start.9
  31.7 2.0 convolution_convert_fusion
  33.6 7.1 %all-to-all-start = ((bf16[16,16,384]{2,1,0:T(8,128)(2,1)}), bf16[16,16,384]{2,1,0:T(8,128)(2,1)S(1)}, u32[]{:S(2)}, u32[]{:S(2)}) async-start(bf16[16,16,384]{2,1,0:T(8,128)(2,1)} %bitcast), calls=%async_computation | async-start | bytes 393216 | tf_op jit(solution)/shard_map/all_to_all | solution.py:656
  40.8 0.0 copy-done.6
  40.8 0.0 copy-done.8
  40.8 0.7 copy.18.targets
  41.5 0.0 copy-done.9
  41.5 0.1 fusion
  41.6 0.1 multiply_cosine_fusion
  41.7 7.1 %all-to-all-done = bf16[16,16,384]{2,1,0:T(8,128)(2,1)S(1)} async-done(((bf16[16,16,384]{2,1,0:T(8,128)(2,1)}), bf16[16,16,384]{2,1,0:T(8,128)(2,1)S(1)}, u32[]{:S(2)}, u32[]{:S(2)}) %all-to-all-start) | async-done | bytes 196640 | tf_op jit(solution)/shard_map/all_to_all | solution.py:656
  48.9 0.1 copy.20
  48.9 0.1 subtract_convert_fusion.1
  49.0 0.1 subtract_convert_fusion
  49.2 0.1 pad_maximum_fusion.1
  49.3 0.1 pad_maximum_fusion.query
  49.5 0.0 copy-start.7
  49.5 0.0 copy-start.5
  49.5 0.0 copy-start.4
  49.5 21.8 %shard_map.141 = bf16[16,32,128]{2,1,0:T(8,128)(2,1)S(1)} custom-call(s32[16]{0:T(128)S(1)} %get-tuple-element.7.positions, bf16[16,32,128]{2,1,0:T(8,128)(2,1)S(1)} %pad_maximum_fusion.query, bf16[16,32,128]{2,1,0:T(8,128)(2,1)S(1)} %bitcast.22, bf16[16,32,128]{2,1,0:T(8,128)(2,1)S(1)} %bitcast.23, bf16[16,512,2048]{2,1,0:T(8,128)(2,1)} %cache.1), custom_call_target="tpu_custom_call" | custom-call | tf_op jit(solution)/shard_map/pallas_call | solution.py:605
  71.4 0.7 copy.16
  72.1 3.5 %all-to-all-start.1 = ((bf16[16,16,256]{2,0,1:T(8,128)(2,1)}), bf16[16,16,256]{2,0,1:T(8,128)(2,1)S(1)}, u32[]{:S(2)}, u32[]{:S(2)}) async-start(bf16[16,16,256]{2,0,1:T(8,128)(2,1)} %copy.16), calls=%async_computation.1 | async-start | bytes 262144 | tf_op jit(solution)/shard_map/all_to_all | solution.py:658
  75.7 0.0 copy-done.7
  75.7 0.6 constant_dynamic-slice_fusion.scale
  76.3 7.1 %all-to-all-done.1 = bf16[16,16,256]{2,0,1:T(8,128)(2,1)S(1)} async-done(((bf16[16,16,256]{2,0,1:T(8,128)(2,1)}), bf16[16,16,256]{2,0,1:T(8,128)(2,1)S(1)}, u32[]{:S(2)}, u32[]{:S(2)}) %all-to-all-start.1) | async-done | bytes 131104 | tf_op jit(solution)/shard_map/all_to_all | solution.py:658
  83.4 0.0 copy-start.3
  83.4 0.0 copy-done.5
  83.4 0.8 broadcast_in_dim.15.fast_in
  84.3 0.0 copy-done.4
  84.3 0.8 broadcast_in_dim.14.gains
  85.1 0.7 broadcast_in_dim.16.fast_hidden
  85.7 0.0 copy-done.3
  85.7 0.0 copy-start.1
  85.7 118.9 %shard_map.142 = (bf16[128,4096]{1,0:T(8,128)(2,1)}, f32[1,128]{1,0:T(1,128)}) custom-call(bf16[256,256]{1,0:T(8,128)(2,1)} %bitcast.29, bf16[256,4096]{1,0:T(8,128)(2,1)} %w_out.1, bf16[16,4096]{1,0:T(8,128)(2,1)} %stream.3, f32[3,8,4096]{2,1,0:T(8,128)} %broadcast_in_dim.14.gains, f32[2,2,8,4096]{3,2,1,0:T(8,128)} %broadcast_in_dim.15.fast_in, ...), custom_call_target="tpu_custom_call" | custom-call | bytes 67108864 | tf_op jit(solution)/shard_map/pallas_call | solution.py:531
  204.6 2.3 %copy.25 = bf16[128,4096]{1,0:T(8,128)(2,1)} copy(bf16[128,4096]{1,0:T(8,128)(2,1)} %get-tuple-element.18) | data formatting | bytes 2097152
  206.9 1.2 copy.26
  208.0 0.0 copy-done.1
  (10 shorter events, 0.2 us)
Async XLA Ops:
  0.6 31.0 %copy-start = (bf16[4096,384]{1,0:T(8,128)(2,1)S(1)}, bf16[4096,384]{1,0:T(8,128)(2,1)}, u32[]{:S(2)}) copy-start(bf16[4096,384]{1,0:T(8,128)(2,1)} %param.18) | copy-start | bytes 9437188
  1.7 0.9 copy-start.2
  31.6 9.1 %copy-start.6 = (f32[2,3,896]{2,0,1:T(2,128)S(1)}, f32[2,3,896]{2,0,1:T(2,128)}, u32[]{:S(2)}) copy-start(f32[2,3,896]{2,0,1:T(2,128)} %param.24) | copy-start | bytes 64516
  31.6 9.1 %copy-start.8 = (s32[128]{0:T(128)S(1)}, s32[128]{0:T(128)}, u32[]{:S(2)}) copy-start(s32[128]{0:T(128)} %param.16) | copy-start | bytes 1540
  31.6 9.9 %copy-start.9 = (s32[128]{0:T(128)S(1)}, s32[128]{0:T(128)}, u32[]{:S(2)}) copy-start(s32[128]{0:T(128)} %param.15) | copy-start | bytes 1540
  33.6 15.2 %all-to-all-start = ((bf16[16,16,384]{2,1,0:T(8,128)(2,1)}), bf16[16,16,384]{2,1,0:T(8,128)(2,1)S(1)}, u32[]{:S(2)}, u32[]{:S(2)}) async-start(bf16[16,16,384]{2,1,0:T(8,128)(2,1)} %bitcast), calls=%async_computation | async-start | bytes 393216 | tf_op jit(solution)/shard_map/all_to_all | solution.py:656
  49.5 26.1 %copy-start.7 = (f32[2,4096]{1,0:T(2,128)S(1)}, f32[2,4096]{1,0:T(2,128)}, u32[]{:S(2)}) copy-start(f32[2,4096]{1,0:T(2,128)} %param.25) | copy-start | bytes 98308
  49.5 33.9 %copy-start.5 = (f32[2,2,4096]{2,1,0:T(2,128)S(1)}, f32[2,2,4096]{2,1,0:T(2,128)}, u32[]{:S(2)}) copy-start(f32[2,2,4096]{2,1,0:T(2,128)} %param.23) | copy-start | bytes 196612
  49.5 34.7 %copy-start.4 = (f32[3,4096]{1,0:T(4,128)S(1)}, f32[3,4096]{1,0:T(4,128)}, u32[]{:S(2)}) copy-start(f32[3,4096]{1,0:T(4,128)} %param.17) | copy-start | bytes 147460
  72.1 11.3 %all-to-all-start.1 = ((bf16[16,16,256]{2,0,1:T(8,128)(2,1)}), bf16[16,16,256]{2,0,1:T(8,128)(2,1)S(1)}, u32[]{:S(2)}, u32[]{:S(2)}) async-start(bf16[16,16,256]{2,0,1:T(8,128)(2,1)} %copy.16), calls=%async_computation.1 | async-start | bytes 262144 | tf_op jit(solution)/shard_map/all_to_all | solution.py:658
  83.4 2.3 %copy-start.3 = (bf16[16,16,256]{2,0,1:T(8,128)(2,1)}, bf16[16,16,256]{2,0,1:T(8,128)(2,1)S(1)}, u32[]{:S(2)}) copy-start(bf16[16,16,256]{2,0,1:T(8,128)(2,1)S(1)} %all-to-all-done.1) | copy-start | bytes 393220
  85.7 122.3 %copy-start.1 = (bf16[4096,384]{1,0:T(8,128)(2,1)S(1)}, bf16[4096,384]{1,0:T(8,128)(2,1)}, u32[]{:S(2)}) copy-start(bf16[4096,384]{1,0:T(8,128)(2,1)} %param.18) | copy-start | bytes 9437188
